TPU v7x, 32 devices: a whole 2x2x4 slice. The times are simulated.
32 devices in a mesh: grp: 8 (over y, x, core), wrk: 4 (over z).
Axes of the slice: x: 2, y: 2, z: 4, core: 2. Of those that a mesh axis runs over, the one named last changes fastest.
Arguments:
- mono_ham: bfloat16 [32, 256, 256], P(('grp', 'wrk')), as said below
- polymer_members: int32 [32, 3], P(('grp', 'wrk')), may hold values from -1 to 31, as said below
- polymer_coupling: bfloat16 [32, 3, 256, 256], P(('grp', 'wrk')), may hold values from -0.29882812 to 0.29882812
Outputs:
- density: float32 [32, 256, 256], P(('grp', 'wrk'))
Inputs may be any that keep to these rules, and one draw needn't show every extreme that they name: `mono_ham`: each block is symmetric. `polymer_members`: row p lists distinct members: the first is monomer p itself; the second is another monomer of p's group (p // 4) or a monomer of the next group ((p // 4 + 1) mod 8); the third is -1 for a dimer, else a monomer of the next group.
All inputs are finite; a program needn't handle non-finite values.
Results may differ from a plain program's by a relative error of at most 0.012.
Values may be sent and summed in bfloat16 or wider, within the bound.
No kernel may reach another device: no remote copies, remote signals or barrier semaphores. Data moves between devices by JAX's collectives and lax.ppermute only.
A program may use at most 64 MiB of HBM per device.

v0:
```python
import functools

import jax
import jax.numpy as jnp
from jax import lax
from jax.experimental import pallas as pl
from jax.experimental.pallas import tpu as pltpu
from jax.sharding import PartitionSpec as P


F32 = jnp.float32
BF16 = jnp.bfloat16
PAD = 8


def from_behind(block, axis, distance):
    devices = range(lax.axis_size(axis))
    route = [((i - distance) % len(devices), i) for i in devices]
    return lax.ppermute(block, axis, route)


def dot(a, b):
    return jnp.dot(a, b, preferred_element_type=F32)


def grid_masks(half):
    row = lax.broadcasted_iota(jnp.int32, (half, half), 0)
    col = lax.broadcasted_iota(jnp.int32, (half, half), 1)
    return row, col


def eye(n):
    row, col = grid_masks(n)
    return jnp.where(row == col, 1.0, 0.0)


def pack_into(ref, index, block, code=None):
    n = block.shape[-1]
    half = n // 2
    row, col = grid_masks(half)
    low = block[half:, half:]
    folded = jnp.where(row >= col, block[:half, :half], low)
    diagonal = jnp.sum(jnp.where(row == col, low, 0.0), axis=0, keepdims=True)
    ref[index, :half, :] = folded.astype(BF16)
    ref[index, half:n, :] = block[:half, half:].astype(BF16)
    tail = jnp.broadcast_to(diagonal, (PAD, half))
    if code is not None:
        line = lax.broadcasted_iota(jnp.int32, (PAD, half), 0)
        tail = jnp.where(line == 0, tail, code)
    ref[index, n:, :] = tail.astype(BF16)


def unpack(packed):
    half = packed.shape[-1]
    folded, corner, diagonal = packed[:half], packed[half : 2 * half], packed[2 * half : 2 * half + 1]
    row, col = grid_masks(half)
    turned = folded.T
    first = jnp.where(row >= col, folded, turned)
    last = jnp.where(row < col, folded, jnp.where(row > col, turned, diagonal))
    return first, corner, corner.T, last


def purified(low):
    square = dot(low, low)
    density = 3.0 * square - 2.0 * dot(square.astype(BF16), low)
    low = density.astype(BF16)
    square = dot(low, low)
    return 3.0 * square - 2.0 * dot(square.astype(BF16), low)


def pack_kernel(ham, out, own):
    n = ham.shape[-1]
    block = 0.5 * eye(n) - 0.35 * ham[0].astype(F32)
    pack_into(out, 0, block)
    own[...] = block.astype(BF16)


def early_kernel(members, own_ref, coupling, frame, known, rows, *, workers, groups):
    n = own_ref.shape[-1]
    group = lax.axis_index("grp")
    slot = lax.axis_index("wrk")
    following = lax.rem(group + 1, groups)
    second, last = members[0, 1], members[0, 2]
    line = 0

    def put(value):
        nonlocal line
        rows[line, :] = jnp.full((n // 2,), value, F32)
        line += 1

    for k in range(1, workers):
        mate = group * workers + lax.rem(slot + k, workers)
        put(jnp.where(second == mate, 1.0, 0.0))
    for member in (second, last):
        for k in range(workers):
            mate = following * workers + lax.rem(slot + k, workers)
            put(jnp.where(member == mate, 1.0, 0.0))
    inside = (second >= group * workers) & (second < (group + 1) * workers)
    second_slot = lax.rem(second, workers).astype(F32)
    put(jnp.where(inside, second_slot, -1.0))
    put(jnp.where(inside, -1.0, second_slot))
    put(jnp.where(last >= 0, lax.rem(last, workers), -1).astype(F32))
    for k in range(workers):
        put(lax.rem(slot + workers - k, workers).astype(F32))
    own = own_ref[...]
    third = jnp.where(last >= 0, 1.0, 0.0)
    c01 = -0.35 * coupling[0, 0].astype(F32)
    c02 = -0.35 * coupling[0, 1].astype(F32) * third
    c12 = -0.35 * coupling[0, 2].astype(F32) * third
    frame[:n, :n] = own
    frame[:n, n : 2 * n] = c01.astype(BF16)
    frame[:n, 2 * n :] = c02.astype(BF16)
    frame[n : 2 * n, :n] = c01.T.astype(BF16)
    frame[n : 2 * n, n : 2 * n] = jnp.zeros((n, n), BF16)
    frame[n : 2 * n, 2 * n :] = c12.astype(BF16)
    frame[2 * n :, :n] = c02.T.astype(BF16)
    frame[2 * n :, n : 2 * n] = c12.T.astype(BF16)
    frame[2 * n :, 2 * n :] = jnp.zeros((n, n), BF16)
    for j in range(3):
        part = slice(j * n, (j + 1) * n)
        known[: (j + 1) * n, part] = dot(frame[: (j + 1) * n, :], frame[:, part])


def main_kernel(*refs, workers):
    own = refs[: workers - 1]
    following = refs[workers - 1 : 2 * workers - 1]
    first, known, rows, going, frame, crossed, low = refs[2 * workers - 1 :]
    n = known.shape[-1] // 3
    half = n // 2
    base = 3 * workers - 1

    def part(i):
        return slice(i * n, (i + 1) * n)

    def chosen(candidates, first_row):
        total = jnp.zeros((n + PAD, half), F32)
        for c, ref in enumerate(candidates):
            total = jnp.where(rows[first_row + c : first_row + c + 1, :] > 0.5, ref[0].astype(F32), total)
        return total

    members = []
    for packed in (chosen(own + following, 0), chosen(following, 2 * workers - 1)):
        a, b, c, d = unpack(packed)
        block = jnp.concatenate([jnp.concatenate([a, b], 1), jnp.concatenate([c, d], 1)], 0)
        members.append(block)
    second, last = [block.astype(BF16) for block in members]
    blocks = {(i, j): first[part(i), part(j)] for i in range(3) for j in range(3)}
    blocks[1, 1], blocks[2, 2] = second, last

    def rectangle(table, down, across):
        return jnp.concatenate([jnp.concatenate([table[i, j] for j in across], 1) for i in down], 0)

    square = {(i, j): known[part(i), part(j)] for j in range(3) for i in range(j + 1)}
    extra = dot(rectangle(blocks, (0, 1), (1,)), second)
    square[0, 1] += extra[:n]
    square[1, 1] += extra[n:]
    extra = dot(rectangle(blocks, (0, 1, 2), (2,)), last)
    square[0, 2] += extra[:n]
    square[1, 2] += extra[n : 2 * n] + dot(second, blocks[1, 2])
    square[2, 2] += extra[2 * n :]
    for (i, j), value in square.items():
        low[part(i), part(j)] = value.astype(BF16)
        if i < j:
            low[part(j), part(i)] = value.T.astype(BF16)
    for j in range(3):
        product = dot(rectangle(blocks, range(j + 1), range(3)), low[:, part(j)])
        for i in range(j + 1):
            value = 3.0 * square[i, j] - 2.0 * product[part(i)]
            frame[part(i), part(j)] = value.astype(BF16)
            if i < j:
                frame[part(j), part(i)] = value.T.astype(BF16)
    square = {}
    for j in (1, 2):
        product = dot(frame[: (j + 1) * n, :], frame[:, part(j)])
        for i in range(j + 1):
            square[i, j] = product[part(i)]
            low[part(i), part(j)] = square[i, j].astype(BF16)
            if i == 1 and j == 2:
                low[part(j), part(i)] = square[i, j].T.astype(BF16)
    crossed[0] = square[0, 1].T.astype(BF16)
    crossed[1] = square[0, 2].T.astype(BF16)
    for s in (1, 2):
        density = 3.0 * square[s, s] - 2.0 * dot(frame[part(s), :], low[:, part(s)])
        pack_into(going, s - 1, density - members[s - 1], rows[base + s : base + s + 1, :])


def own_kernel(own, frame, crossed, mine, delta):
    n = mine.shape[-1]
    delta[...] = own[...].astype(F32) - purified(own[...])
    square = dot(frame[:n, :], frame[:, :n])
    low = jnp.concatenate([square.astype(BF16), crossed[0], crossed[1]], 0)
    mine[...] = 3.0 * square - 2.0 * dot(frame[:n, :], low)


def collect_kernel(back, going, rows, *outs, workers):
    half = back.shape[-1]
    n = 2 * half
    base = 3 * workers + 2
    line = lax.broadcasted_iota(jnp.int32, (n + PAD, half), 0)
    pieces = []
    for piece in (back[0], back[1]):
        piece = piece.astype(F32)
        pieces.append((piece, piece[n + 1 : n + 2, :]))
    pieces.append((going[0].astype(F32), rows[base - 3 : base - 2, :]))
    pieces = [(jnp.where(line > n, 1.0, piece), code) for piece, code in pieces]
    for k in range(workers):
        slot = rows[base + k : base + k + 1, :]
        total = jnp.zeros((n + PAD, half), F32)
        for piece, code in pieces:
            total = total + jnp.where(code == slot, piece, 0.0)
        outs[k][0] = total.astype(BF16)


def finish_kernel(*refs):
    *packed, mine, delta, out = refs
    n = mine.shape[-1]
    half = n // 2
    total = packed[0][0].astype(F32)
    for ref in packed[1:]:
        total = total + ref[0].astype(F32)
    count = total[n + 1 : n + 2, :]
    top, bottom = slice(0, half), slice(half, n)
    for value, down, across in zip(unpack(total), (top, top, bottom, bottom), (top, bottom, top, bottom)):
        out[0, down, across] = mine[down, across] + count * delta[down, across] + value


def call(kernel, operands, outs, flops=0, scratch=(), spaces=None, limit=24):
    vmem = pl.BlockSpec(memory_space=pltpu.VMEM)
    specs = [vmem] * len(operands)
    for at, space in (spaces or {}).items():
        specs[at] = pl.BlockSpec(memory_space=space)
    return pl.pallas_call(
        kernel,
        in_specs=specs,
        out_specs=[vmem] * len(outs),
        out_shape=[jax.ShapeDtypeStruct(*out) for out in outs],
        scratch_shapes=scratch,
        cost_estimate=pl.CostEstimate(flops=flops, bytes_accessed=0, transcendentals=0),
        compiler_params=pltpu.CompilerParams(vmem_limit_bytes=limit * 1024 * 1024),
    )(*operands)


def in_order(workers):
    return list(range(workers - 1, 0, -1))


def out_order(workers):
    return list(range(workers - 1, 0, -1))


def step(mono_ham, polymer_members, polymer_coupling):
    workers = lax.axis_size("wrk")
    groups = lax.axis_size("grp")
    n = mono_ham.shape[-1]
    tall, wide = n + PAD, n // 2
    packed, own = call(pack_kernel, (mono_ham,), [((1, tall, wide), BF16), ((n, n), BF16)], flops=1000)
    mates = {}
    for k in in_order(workers):
        mates[k] = from_behind(packed, "wrk", -k)
    following = []
    for k in range(workers):
        following.append(from_behind(mates[k] if k else packed, "grp", -1))
    n_rows = 4 * workers + 2
    frame, known, rows = call(
        functools.partial(early_kernel, workers=workers, groups=groups),
        (polymer_members, own, polymer_coupling),
        [((3 * n, 3 * n), BF16), ((3 * n, 3 * n), F32), ((n_rows, wide), F32)],
        flops=2 * 18 * n**3,
        spaces={0: pltpu.SMEM},
    )
    going, frame, crossed = call(
        functools.partial(main_kernel, workers=workers),
        [mates[k] for k in range(1, workers)] + following + [frame, known, rows],
        [((2, tall, wide), BF16), ((3 * n, 3 * n), BF16), ((2, n, n), BF16)],
        flops=2 * 45 * n**3,
        scratch=[pltpu.VMEM((3 * n, 3 * n), BF16)],
    )
    back = from_behind(going, "grp", 1)
    mine, delta = call(own_kernel, (own, frame, crossed), [((n, n), F32)] * 2, flops=2 * 10 * n**3)
    sums = call(
        functools.partial(collect_kernel, workers=workers),
        (back, going, rows),
        [((1, tall, wide), BF16)] * workers,
        flops=1000,
    )
    received = []
    for k in out_order(workers):
        received.append(from_behind(sums[k], "wrk", -k))
    (density,) = call(finish_kernel, [sums[0]] + received + [mine, delta], [((1, n, n), F32)], flops=1000)
    return density


def solution(mesh):
    placed = (
        P(("grp", "wrk"), None, None),
        P(("grp", "wrk"), None),
        P(("grp", "wrk"), None, None, None),
    )
    return jax.shard_map(step, mesh=mesh, in_specs=placed, out_specs=P(("grp", "wrk"), None, None), check_vma=False)
```

profile of v0, /device:TPU:0, one launch (start us, length us, event | category | flops | bytes accessed | tf_op | source)
XLA Modules:
  0.0 34.2 jit_solution(2311047368366052497)
XLA Ops:
  0.0 0.0 copy-start
  0.0 0.9 %copy-done = bf16[1,256,256]{2,1,0:T(8,128)(2,1)S(1)} copy-done((bf16[1,256,256]{2,1,0:T(8,128)(2,1)S(1)}, bf16[1,256,256]{2,1,0:T(8,128)(2,1)}, u32[]{:S(2)}) %copy-start) | copy-done | bytes 131096
  0.9 0.1 shard_map.37
  1.0 3.1 %collective-permute-start.2 = (bf16[1,264,128]{2,1,0:T(8,128)(2,1)S(1)}, bf16[1,264,128]{2,1,0:T(8,128)(2,1)S(1)}, u32[]{:S(2)}, u32[]{:S(2)}) collective-permute-start(bf16[1,264,128]{2,1,0:T(8,128)(2,1)S(1)} %get-tuple-element.19), channel_id=1, source_target_pairs={{3,0},{0,1},{1,2},{2,3},{7,4},{4,5},{5,6},{6,7},{11,8},{8,9},{9,10... | collective-permute-start | bytes 202760 | tf_op jit(solution)/shard_map/ppermute | solution.py:19
  4.1 2.6 %collective-permute-start.1 = (bf16[1,264,128]{2,1,0:T(8,128)(2,1)S(1)}, bf16[1,264,128]{2,1,0:T(8,128)(2,1)S(1)}, u32[]{:S(2)}, u32[]{:S(2)}) collective-permute-start(bf16[1,264,128]{2,1,0:T(8,128)(2,1)S(1)} %get-tuple-element.19), channel_id=1, source_target_pairs={{2,0},{3,1},{0,2},{1,3},{6,4},{7,5},{4,6},{5,7},{10,8},{11,9},{8,1... | collective-permute-start | bytes 202760 | tf_op jit(solution)/shard_map/ppermute | solution.py:19
  6.7 1.3 %collective-permute-start = (bf16[1,264,128]{2,1,0:T(8,128)(2,1)S(1)}, bf16[1,264,128]{2,1,0:T(8,128)(2,1)S(1)}, u32[]{:S(2)}, u32[]{:S(2)}) collective-permute-start(bf16[1,264,128]{2,1,0:T(8,128)(2,1)S(1)} %get-tuple-element.19), channel_id=1, source_target_pairs={{1,0},{2,1},{3,2},{0,3},{5,4},{6,5},{7,6},{4,7},{9,8},{10,9},{11,1... | collective-permute-start | bytes 202760 | tf_op jit(solution)/shard_map/ppermute | solution.py:19
  8.0 1.0 %collective-permute-start.3 = (bf16[1,264,128]{2,1,0:T(8,128)(2,1)S(1)}, bf16[1,264,128]{2,1,0:T(8,128)(2,1)S(1)}, u32[]{:S(2)}, u32[]{:S(2)}) collective-permute-start(bf16[1,264,128]{2,1,0:T(8,128)(2,1)S(1)} %get-tuple-element.19), channel_id=1, source_target_pairs={{4,0},{8,4},{12,8},{16,12},{20,16},{24,20},{28,24},{0,28},{5,1},{9... | collective-permute-start | bytes 202760 | tf_op jit(solution)/shard_map/ppermute | solution.py:19
  9.1 0.0 collective-permute-done.2.refs_2_
  9.1 1.5 %collective-permute-start.6 = (bf16[1,264,128]{2,1,0:T(8,128)(2,1)S(1)}, bf16[1,264,128]{2,1,0:T(8,128)(2,1)S(1)}, u32[]{:S(2)}, u32[]{:S(2)}) collective-permute-start(bf16[1,264,128]{2,1,0:T(8,128)(2,1)S(1)} %collective-permute-done.2.refs_2_), channel_id=1, source_target_pairs={{4,0},{8,4},{12,8},{16,12},{20,16},{24,20},{28,24},{0,28},{5,1},{9... | collective-permute-start | bytes 202760 | tf_op jit(solution)/shard_map/ppermute | solution.py:19
  10.6 0.7 %collective-permute-done.1.refs_1_ = bf16[1,264,128]{2,1,0:T(8,128)(2,1)S(1)} collective-permute-done((bf16[1,264,128]{2,1,0:T(8,128)(2,1)S(1)}, bf16[1,264,128]{2,1,0:T(8,128)(2,1)S(1)}, u32[]{:S(2)}, u32[]{:S(2)}) %collective-permute-start.1) | collective-permute-done | bytes 67616 | tf_op jit(solution)/shard_map/ppermute | solution.py:19
  11.3 1.7 %collective-permute-start.5 = (bf16[1,264,128]{2,1,0:T(8,128)(2,1)S(1)}, bf16[1,264,128]{2,1,0:T(8,128)(2,1)S(1)}, u32[]{:S(2)}, u32[]{:S(2)}) collective-permute-start(bf16[1,264,128]{2,1,0:T(8,128)(2,1)S(1)} %collective-permute-done.1.refs_1_), channel_id=1, source_target_pairs={{4,0},{8,4},{12,8},{16,12},{20,16},{24,20},{28,24},{0,28},{5,1},{9... | collective-permute-start | bytes 202760 | tf_op jit(solution)/shard_map/ppermute | solution.py:19
  13.0 0.0 collective-permute-done.refs_0_
  13.0 1.1 %collective-permute-start.4 = (bf16[1,264,128]{2,1,0:T(8,128)(2,1)S(1)}, bf16[1,264,128]{2,1,0:T(8,128)(2,1)S(1)}, u32[]{:S(2)}, u32[]{:S(2)}) collective-permute-start(bf16[1,264,128]{2,1,0:T(8,128)(2,1)S(1)} %collective-permute-done.refs_0_), channel_id=1, source_target_pairs={{4,0},{8,4},{12,8},{16,12},{20,16},{24,20},{28,24},{0,28},{5,1},{9... | collective-permute-start | bytes 202760 | tf_op jit(solution)/shard_map/ppermute | solution.py:19
  14.0 0.0 copy-start.1
  14.0 1.0 %copy-done.1 = bf16[1,3,256,256]{3,2,1,0:T(8,128)(2,1)S(1)} copy-done((bf16[1,3,256,256]{3,2,1,0:T(8,128)(2,1)S(1)}, bf16[1,3,256,256]{3,2,1,0:T(8,128)(2,1)}, u32[]{:S(2)}) %copy-start.1) | copy-done | bytes 393240
  15.0 0.0 copy-start.2
  15.0 0.7 %copy-done.2 = s32[1,3]{1,0:T(1,128)S(1)} copy-done((s32[1,3]{1,0:T(1,128)S(1)}, s32[1,3]{1,0:T(1,128)}, u32[]{:S(2)}) %copy-start.2) | copy-done | bytes 36
  15.7 1.4 %shard_map.38 = (bf16[768,768]{1,0:T(8,128)(2,1)S(1)}, f32[768,768]{1,0:T(8,128)S(1)}, f32[18,128]{1,0:T(8,128)S(1)}) custom-call(s32[1,3]{1,0:T(1,128)S(1)} %copy-done.2, bf16[256,256]{1,0:T(8,128)(2,1)S(1)} %get-tuple-element.20.own_ref.own, bf16[1,3,256,256]{3,2,1,0:T(8,128)(2,1)S(1)} %copy-done.1), custom_call_target="tpu_custom_call" | custom-call | flops 603979776 | tf_op jit(solution)/shard_map/pallas_call | solution.py:232
  17.1 0.0 collective-permute-done.3.refs_3_
  17.1 0.0 collective-permute-done.6.refs_6_
  17.1 0.0 collective-permute-done.5.refs_5_
  17.1 0.0 collective-permute-done.4.refs_4_
  17.1 2.4 %shard_map.39 = (bf16[2,264,128]{2,1,0:T(8,128)(2,1)S(1)}, bf16[768,768]{1,0:T(8,128)(2,1)S(1)}, bf16[2,256,256]{2,1,0:T(8,128)(2,1)S(1)}) custom-call(bf16[1,264,128]{2,1,0:T(8,128)(2,1)S(1)} %collective-permute-done.refs_0_, bf16[1,264,128]{2,1,0:T(8,128)(2,1)S(1)} %collective-permute-done.1.refs_1_, ...), custom_call_target="tpu_custom_call" | custom-call | flops 1509949440 | tf_op jit(solution)/shard_map/pallas_call | solution.py:232
  19.5 0.1 collective-permute-start.7
  19.6 5.3 %collective-permute-done.7.back = bf16[2,264,128]{2,1,0:T(8,128)(2,1)S(1)} collective-permute-done((bf16[2,264,128]{2,1,0:T(8,128)(2,1)S(1)}, bf16[2,264,128]{2,1,0:T(8,128)(2,1)S(1)}, u32[]{:S(2)}, u32[]{:S(2)}) %collective-permute-start.7) | collective-permute-done | bytes 135200 | tf_op jit(solution)/shard_map/ppermute | solution.py:19
  24.9 0.1 shard_map.40
  25.0 1.0 %collective-permute-start.8 = (bf16[1,264,128]{2,1,0:T(8,128)(2,1)S(1)}, bf16[1,264,128]{2,1,0:T(8,128)(2,1)S(1)}, u32[]{:S(2)}, u32[]{:S(2)}) collective-permute-start(bf16[1,264,128]{2,1,0:T(8,128)(2,1)S(1)} %get-tuple-element.26), channel_id=1, source_target_pairs={{3,0},{0,1},{1,2},{2,3},{7,4},{4,5},{5,6},{6,7},{11,8},{8,9},{9,10... | collective-permute-start | bytes 202760 | tf_op jit(solution)/shard_map/ppermute | solution.py:19
  26.0 2.7 %collective-permute-start.9 = (bf16[1,264,128]{2,1,0:T(8,128)(2,1)S(1)}, bf16[1,264,128]{2,1,0:T(8,128)(2,1)S(1)}, u32[]{:S(2)}, u32[]{:S(2)}) collective-permute-start(bf16[1,264,128]{2,1,0:T(8,128)(2,1)S(1)} %get-tuple-element.27), channel_id=1, source_target_pairs={{2,0},{3,1},{0,2},{1,3},{6,4},{7,5},{4,6},{5,7},{10,8},{11,9},{8,1... | collective-permute-start | bytes 202760 | tf_op jit(solution)/shard_map/ppermute | solution.py:19
  28.8 0.2 collective-permute-start.10
  28.9 1.0 %shard_map.41 = (f32[256,256]{1,0:T(8,128)S(1)}, f32[256,256]{1,0:T(8,128)S(1)}) custom-call(bf16[256,256]{1,0:T(8,128)(2,1)S(1)} %get-tuple-element.20.own_ref.own, bf16[768,768]{1,0:T(8,128)(2,1)S(1)} %get-tuple-element.29.frame, bf16[2,256,256]{2,1,0:T(8,128)(2,1)S(1)} %get-tuple-element.30.crossed), custom_call_target="tpu_custom_call" | custom-call | flops 335544320 | tf_op jit(solution)/shard_map/pallas_call | solution.py:232
  30.0 1.3 %collective-permute-done.8.refs_1_ = bf16[1,264,128]{2,1,0:T(8,128)(2,1)S(1)} collective-permute-done((bf16[1,264,128]{2,1,0:T(8,128)(2,1)S(1)}, bf16[1,264,128]{2,1,0:T(8,128)(2,1)S(1)}, u32[]{:S(2)}, u32[]{:S(2)}) %collective-permute-start.8) | collective-permute-done | bytes 67616 | tf_op jit(solution)/shard_map/ppermute | solution.py:19
  31.3 1.4 %collective-permute-done.9.refs_2_ = bf16[1,264,128]{2,1,0:T(8,128)(2,1)S(1)} collective-permute-done((bf16[1,264,128]{2,1,0:T(8,128)(2,1)S(1)}, bf16[1,264,128]{2,1,0:T(8,128)(2,1)S(1)}, u32[]{:S(2)}, u32[]{:S(2)}) %collective-permute-start.9) | collective-permute-done | bytes 67616 | tf_op jit(solution)/shard_map/ppermute | solution.py:19
  32.7 0.7 %collective-permute-done.10.refs_3_ = bf16[1,264,128]{2,1,0:T(8,128)(2,1)S(1)} collective-permute-done((bf16[1,264,128]{2,1,0:T(8,128)(2,1)S(1)}, bf16[1,264,128]{2,1,0:T(8,128)(2,1)S(1)}, u32[]{:S(2)}, u32[]{:S(2)}) %collective-permute-start.10) | collective-permute-done | bytes 67616 | tf_op jit(solution)/shard_map/ppermute | solution.py:19
  33.4 0.8 %shard_map.42 = f32[1,256,256]{2,1,0:T(8,128)} custom-call(bf16[1,264,128]{2,1,0:T(8,128)(2,1)S(1)} %get-tuple-element.25.refs_0_, bf16[1,264,128]{2,1,0:T(8,128)(2,1)S(1)} %collective-permute-done.8.refs_1_, bf16[1,264,128]{2,1,0:T(8,128)(2,1)S(1)} %collective-permute-done.9.refs_2_, bf16[1,264,128]{2,1,0:T(8,128)(2,1)S(1)} %collective-permute-done.10.refs_3_, ...), custom_call_target="tpu_custom_call" | custom-call | flops 1000 | tf_op jit(solution)/shard_map/pallas_call | solution.py:232
Async XLA Ops:
  0.0 0.9 %copy-start = (bf16[1,256,256]{2,1,0:T(8,128)(2,1)S(1)}, bf16[1,256,256]{2,1,0:T(8,128)(2,1)}, u32[]{:S(2)}) copy-start(bf16[1,256,256]{2,1,0:T(8,128)(2,1)} %ham.1) | copy-start | bytes 393220
  1.0 8.1 %collective-permute-start.2 = (bf16[1,264,128]{2,1,0:T(8,128)(2,1)S(1)}, bf16[1,264,128]{2,1,0:T(8,128)(2,1)S(1)}, u32[]{:S(2)}, u32[]{:S(2)}) collective-permute-start(bf16[1,264,128]{2,1,0:T(8,128)(2,1)S(1)} %get-tuple-element.19), channel_id=1, source_target_pairs={{3,0},{0,1},{1,2},{2,3},{7,4},{4,5},{5,6},{6,7},{11,8},{8,9},{9,10... | collective-permute-start | bytes 202760 | tf_op jit(solution)/shard_map/ppermute | solution.py:19
  4.1 7.2 %collective-permute-start.1 = (bf16[1,264,128]{2,1,0:T(8,128)(2,1)S(1)}, bf16[1,264,128]{2,1,0:T(8,128)(2,1)S(1)}, u32[]{:S(2)}, u32[]{:S(2)}) collective-permute-start(bf16[1,264,128]{2,1,0:T(8,128)(2,1)S(1)} %get-tuple-element.19), channel_id=1, source_target_pairs={{2,0},{3,1},{0,2},{1,3},{6,4},{7,5},{4,6},{5,7},{10,8},{11,9},{8,1... | collective-permute-start | bytes 202760 | tf_op jit(solution)/shard_map/ppermute | solution.py:19
  6.7 6.3 %collective-permute-start = (bf16[1,264,128]{2,1,0:T(8,128)(2,1)S(1)}, bf16[1,264,128]{2,1,0:T(8,128)(2,1)S(1)}, u32[]{:S(2)}, u32[]{:S(2)}) collective-permute-start(bf16[1,264,128]{2,1,0:T(8,128)(2,1)S(1)} %get-tuple-element.19), channel_id=1, source_target_pairs={{1,0},{2,1},{3,2},{0,3},{5,4},{6,5},{7,6},{4,7},{9,8},{10,9},{11,1... | collective-permute-start | bytes 202760 | tf_op jit(solution)/shard_map/ppermute | solution.py:19
  8.0 9.1 %collective-permute-start.3 = (bf16[1,264,128]{2,1,0:T(8,128)(2,1)S(1)}, bf16[1,264,128]{2,1,0:T(8,128)(2,1)S(1)}, u32[]{:S(2)}, u32[]{:S(2)}) collective-permute-start(bf16[1,264,128]{2,1,0:T(8,128)(2,1)S(1)} %get-tuple-element.19), channel_id=1, source_target_pairs={{4,0},{8,4},{12,8},{16,12},{20,16},{24,20},{28,24},{0,28},{5,1},{9... | collective-permute-start | bytes 202760 | tf_op jit(solution)/shard_map/ppermute | solution.py:19
  9.1 8.0 %collective-permute-start.6 = (bf16[1,264,128]{2,1,0:T(8,128)(2,1)S(1)}, bf16[1,264,128]{2,1,0:T(8,128)(2,1)S(1)}, u32[]{:S(2)}, u32[]{:S(2)}) collective-permute-start(bf16[1,264,128]{2,1,0:T(8,128)(2,1)S(1)} %collective-permute-done.2.refs_2_), channel_id=1, source_target_pairs={{4,0},{8,4},{12,8},{16,12},{20,16},{24,20},{28,24},{0,28},{5,1},{9... | collective-permute-start | bytes 202760 | tf_op jit(solution)/shard_map/ppermute | solution.py:19
  11.3 5.8 %collective-permute-start.5 = (bf16[1,264,128]{2,1,0:T(8,128)(2,1)S(1)}, bf16[1,264,128]{2,1,0:T(8,128)(2,1)S(1)}, u32[]{:S(2)}, u32[]{:S(2)}) collective-permute-start(bf16[1,264,128]{2,1,0:T(8,128)(2,1)S(1)} %collective-permute-done.1.refs_1_), channel_id=1, source_target_pairs={{4,0},{8,4},{12,8},{16,12},{20,16},{24,20},{28,24},{0,28},{5,1},{9... | collective-permute-start | bytes 202760 | tf_op jit(solution)/shard_map/ppermute | solution.py:19
  13.0 4.2 %collective-permute-start.4 = (bf16[1,264,128]{2,1,0:T(8,128)(2,1)S(1)}, bf16[1,264,128]{2,1,0:T(8,128)(2,1)S(1)}, u32[]{:S(2)}, u32[]{:S(2)}) collective-permute-start(bf16[1,264,128]{2,1,0:T(8,128)(2,1)S(1)} %collective-permute-done.refs_0_), channel_id=1, source_target_pairs={{4,0},{8,4},{12,8},{16,12},{20,16},{24,20},{28,24},{0,28},{5,1},{9... | collective-permute-start | bytes 202760 | tf_op jit(solution)/shard_map/ppermute | solution.py:19
  14.0 1.0 %copy-start.1 = (bf16[1,3,256,256]{3,2,1,0:T(8,128)(2,1)S(1)}, bf16[1,3,256,256]{3,2,1,0:T(8,128)(2,1)}, u32[]{:S(2)}) copy-start(bf16[1,3,256,256]{3,2,1,0:T(8,128)(2,1)} %coupling.1) | copy-start | bytes 1179652
  15.0 0.7 %copy-start.2 = (s32[1,3]{1,0:T(1,128)S(1)}, s32[1,3]{1,0:T(1,128)}, u32[]{:S(2)}) copy-start(s32[1,3]{1,0:T(1,128)} %members.1) | copy-start | bytes 40
  19.5 5.4 %collective-permute-start.7 = (bf16[2,264,128]{2,1,0:T(8,128)(2,1)S(1)}, bf16[2,264,128]{2,1,0:T(8,128)(2,1)S(1)}, u32[]{:S(2)}, u32[]{:S(2)}) collective-permute-start(bf16[2,264,128]{2,1,0:T(8,128)(2,1)S(1)} %get-tuple-element.24.going), channel_id=1, source_target_pairs={{28,0},{0,4},{4,8},{8,12},{12,16},{16,20},{20,24},{24,28},{29,1},{... | collective-permute-start | bytes 405512 | tf_op jit(solution)/shard_map/ppermute | solution.py:19
  25.0 6.2 %collective-permute-start.8 = (bf16[1,264,128]{2,1,0:T(8,128)(2,1)S(1)}, bf16[1,264,128]{2,1,0:T(8,128)(2,1)S(1)}, u32[]{:S(2)}, u32[]{:S(2)}) collective-permute-start(bf16[1,264,128]{2,1,0:T(8,128)(2,1)S(1)} %get-tuple-element.26), channel_id=1, source_target_pairs={{3,0},{0,1},{1,2},{2,3},{7,4},{4,5},{5,6},{6,7},{11,8},{8,9},{9,10... | collective-permute-start | bytes 202760 | tf_op jit(solution)/shard_map/ppermute | solution.py:19
  26.0 6.7 %collective-permute-start.9 = (bf16[1,264,128]{2,1,0:T(8,128)(2,1)S(1)}, bf16[1,264,128]{2,1,0:T(8,128)(2,1)S(1)}, u32[]{:S(2)}, u32[]{:S(2)}) collective-permute-start(bf16[1,264,128]{2,1,0:T(8,128)(2,1)S(1)} %get-tuple-element.27), channel_id=1, source_target_pairs={{2,0},{3,1},{0,2},{1,3},{6,4},{7,5},{4,6},{5,7},{10,8},{11,9},{8,1... | collective-permute-start | bytes 202760 | tf_op jit(solution)/shard_map/ppermute | solution.py:19
  28.8 4.6 %collective-permute-start.10 = (bf16[1,264,128]{2,1,0:T(8,128)(2,1)S(1)}, bf16[1,264,128]{2,1,0:T(8,128)(2,1)S(1)}, u32[]{:S(2)}, u32[]{:S(2)}) collective-permute-start(bf16[1,264,128]{2,1,0:T(8,128)(2,1)S(1)} %get-tuple-element.28), channel_id=1, source_target_pairs={{1,0},{2,1},{3,2},{0,3},{5,4},{6,5},{7,6},{4,7},{9,8},{10,9},{11,1... | collective-permute-start | bytes 202760 | tf_op jit(solution)/shard_map/ppermute | solution.py:19
where the time goes:
time: 34.4 us; the launch traced here: 34.2 us
  starting transfers between devices  16.3 us (47%)
  waiting for transfers between devices  9.39 us (27%)
  Pallas kernels  5.83 us (17%)
  local copies, waits for them, and re-layouts  2.55 us (7%)
    ppermute x11, starting transfers between devices, from_behind(): return lax.ppermute(block, axis, route)  16.3 us
    ppermute x11, waiting for transfers between devices, from_behind(): return lax.ppermute(block, axis, route)  9.39 us
    pallas_call x6, Pallas kernels, call(): pl.pallas_call(kernel, in_specs=specs, out_specs=[vmem] * len(outs), out_...  5.83 us
    unnamed x6, local copies, waits for them, and re-layouts  2.55 us
  transfers between devices with their start and end apart: 11, of which 5 were waited for; matrix products, arithmetic and copies ran while one was open for 0% of the time, Pallas kernels for 7%

commit v1 on v0

--- a/solution.py
+++ b/solution.py
@@ -13,10 +13,60 @@
 PAD = 8
 
 
-def from_behind(block, axis, distance):
-    devices = range(lax.axis_size(axis))
-    route = [((i - distance) % len(devices), i) for i in devices]
-    return lax.ppermute(block, axis, route)
+def mate(slot, k, workers):
+    return slot ^ k if workers == 4 else lax.rem(slot + k, workers)
+
+
+def pairs(distance, k):
+    groups, workers = lax.axis_size("grp"), lax.axis_size("wrk")
+    for g in range(groups):
+        for w in range(workers):
+            other = w ^ k if workers == 4 else (w + k) % workers
+            yield g * workers + w, (g + distance) % groups * workers + other
+
+
+def from_mate(block, distance, k):
+    return lax.ppermute(block, ("grp", "wrk"), [(there, here) for here, there in pairs(distance, k)])
+
+
+def to_mate(block, distance, k):
+    return lax.ppermute(block, ("grp", "wrk"), list(pairs(distance, k)))
+
+
+def everyone(workers):
+    return [(0, k) for k in range(1, workers)] + [(1, k) for k in range(workers)]
+
+
+def gather_plan(workers):
+    if workers == 4:
+        return [(0, 2, None), (1, 1, None), (0, 1, None), (1, 0, None), (0, 1, 2), (1, 1, 2), (1, 0, 2)]
+    return [(distance, k, None) for distance, k in everyone(workers)]
+
+
+def gather(packed):
+    blocks = {}
+    for distance, k, what in gather_plan(lax.axis_size("wrk")):
+        sent = packed if what is None else blocks[0, what]
+        blocks[distance, k ^ (what or 0)] = from_mate(sent, distance, k)
+    return [blocks[at] for at in everyone(lax.axis_size("wrk"))]
+
+
+def return_plan(workers):
+    if workers == 4:
+        return [(1, 1, 3), (1, 0, 2), (0, 1, 3), (1, 0, 0), (1, 1, 1), (0, 1, 1)]
+    return [(distance, k, k) for distance, k in everyone(workers)]
+
+
+def give_back(pieces):
+    workers = lax.axis_size("wrk")
+    near, far = [], []
+    for distance, k, owner in return_plan(workers):
+        block = to_mate(pieces[distance, owner], distance, k)
+        (near if k == owner else far).append(block)
+    if far:
+        (total,) = call(add_kernel, far + [pieces[0, 2]], [(far[0].shape, BF16)], flops=1000)
+        near.append(to_mate(total, 0, 2))
+    return near
 
 
 def dot(a, b):
@@ -34,20 +84,16 @@
     return jnp.where(row == col, 1.0, 0.0)
 
 
-def pack_into(ref, index, block, code=None):
+def pack(block):
     n = block.shape[-1]
     half = n // 2
     row, col = grid_masks(half)
     low = block[half:, half:]
     folded = jnp.where(row >= col, block[:half, :half], low)
     diagonal = jnp.sum(jnp.where(row == col, low, 0.0), axis=0, keepdims=True)
-    ref[index, :half, :] = folded.astype(BF16)
-    ref[index, half:n, :] = block[:half, half:].astype(BF16)
-    tail = jnp.broadcast_to(diagonal, (PAD, half))
-    if code is not None:
-        line = lax.broadcasted_iota(jnp.int32, (PAD, half), 0)
-        tail = jnp.where(line == 0, tail, code)
-    ref[index, n:, :] = tail.astype(BF16)
+    line = lax.broadcasted_iota(jnp.int32, (PAD, half), 0)
+    tail = jnp.where(line == 0, diagonal, 1.0)
+    return jnp.concatenate([folded, block[:half, half:], tail], 0)
 
 
 def unpack(packed):
@@ -71,7 +117,7 @@
 def pack_kernel(ham, out, own):
     n = ham.shape[-1]
     block = 0.5 * eye(n) - 0.35 * ham[0].astype(F32)
-    pack_into(out, 0, block)
+    out[0] = pack(block).astype(BF16)
     own[...] = block.astype(BF16)
 
 
@@ -80,28 +126,22 @@
     group = lax.axis_index("grp")
     slot = lax.axis_index("wrk")
     following = lax.rem(group + 1, groups)
-    second, last = members[0, 1], members[0, 2]
+    second, last = members[:, 1:2], members[:, 2:3]
     line = 0
 
     def put(value):
         nonlocal line
-        rows[line, :] = jnp.full((n // 2,), value, F32)
+        rows[line : line + 1, :] = jnp.broadcast_to(value, (1, n // 2)).astype(F32)
         line += 1
 
+    def hit(member, member_group, member_slot):
+        return jnp.where(member == member_group * workers + member_slot, 1.0, 0.0)
+
     for k in range(1, workers):
-        mate = group * workers + lax.rem(slot + k, workers)
-        put(jnp.where(second == mate, 1.0, 0.0))
+        put(hit(second, group, mate(slot, k, workers)))
     for member in (second, last):
         for k in range(workers):
-            mate = following * workers + lax.rem(slot + k, workers)
-            put(jnp.where(member == mate, 1.0, 0.0))
-    inside = (second >= group * workers) & (second < (group + 1) * workers)
-    second_slot = lax.rem(second, workers).astype(F32)
-    put(jnp.where(inside, second_slot, -1.0))
-    put(jnp.where(inside, -1.0, second_slot))
-    put(jnp.where(last >= 0, lax.rem(last, workers), -1).astype(F32))
-    for k in range(workers):
-        put(lax.rem(slot + workers - k, workers).astype(F32))
+            put(hit(member, following, mate(slot, k, workers)))
     own = own_ref[...]
     third = jnp.where(last >= 0, 1.0, 0.0)
     c01 = -0.35 * coupling[0, 0].astype(F32)
@@ -124,10 +164,11 @@
 def main_kernel(*refs, workers):
     own = refs[: workers - 1]
     following = refs[workers - 1 : 2 * workers - 1]
-    first, known, rows, going, frame, crossed, low = refs[2 * workers - 1 :]
+    first, known, rows = refs[2 * workers - 1 : 2 * workers + 2]
+    sent = refs[2 * workers + 2 : -3]
+    frame, crossed, low = refs[-3:]
     n = known.shape[-1] // 3
     half = n // 2
-    base = 3 * workers - 1
 
     def part(i):
         return slice(i * n, (i + 1) * n)
@@ -179,9 +220,15 @@
                 low[part(j), part(i)] = square[i, j].T.astype(BF16)
     crossed[0] = square[0, 1].T.astype(BF16)
     crossed[1] = square[0, 2].T.astype(BF16)
+    pieces = []
     for s in (1, 2):
         density = 3.0 * square[s, s] - 2.0 * dot(frame[part(s), :], low[:, part(s)])
-        pack_into(going, s - 1, density - members[s - 1], rows[base + s : base + s + 1, :])
+        pieces.append(pack(density - members[s - 1]))
+    for at, ref in enumerate(sent):
+        value = jnp.where(rows[at : at + 1, :] > 0.5, pieces[0], 0.0)
+        if at >= workers - 1:
+            value = jnp.where(rows[at + workers : at + workers + 1, :] > 0.5, pieces[1], value)
+        ref[0] = value.astype(BF16)
 
 
 def own_kernel(own, frame, crossed, mine, delta):
@@ -192,23 +239,12 @@
     mine[...] = 3.0 * square - 2.0 * dot(frame[:n, :], low)
 
 
-def collect_kernel(back, going, rows, *outs, workers):
-    half = back.shape[-1]
-    n = 2 * half
-    base = 3 * workers + 2
-    line = lax.broadcasted_iota(jnp.int32, (n + PAD, half), 0)
-    pieces = []
-    for piece in (back[0], back[1]):
-        piece = piece.astype(F32)
-        pieces.append((piece, piece[n + 1 : n + 2, :]))
-    pieces.append((going[0].astype(F32), rows[base - 3 : base - 2, :]))
-    pieces = [(jnp.where(line > n, 1.0, piece), code) for piece, code in pieces]
-    for k in range(workers):
-        slot = rows[base + k : base + k + 1, :]
-        total = jnp.zeros((n + PAD, half), F32)
-        for piece, code in pieces:
-            total = total + jnp.where(code == slot, piece, 0.0)
-        outs[k][0] = total.astype(BF16)
+def add_kernel(*refs):
+    *parts, out = refs
+    total = parts[0][...].astype(F32)
+    for ref in parts[1:]:
+        total = total + ref[...].astype(F32)
+    out[...] = total.astype(BF16)
 
 
 def finish_kernel(*refs):
@@ -224,14 +260,11 @@
         out[0, down, across] = mine[down, across] + count * delta[down, across] + value
 
 
-def call(kernel, operands, outs, flops=0, scratch=(), spaces=None, limit=24):
+def call(kernel, operands, outs, flops=0, scratch=(), limit=24):
     vmem = pl.BlockSpec(memory_space=pltpu.VMEM)
-    specs = [vmem] * len(operands)
-    for at, space in (spaces or {}).items():
-        specs[at] = pl.BlockSpec(memory_space=space)
     return pl.pallas_call(
         kernel,
-        in_specs=specs,
+        in_specs=[vmem] * len(operands),
         out_specs=[vmem] * len(outs),
         out_shape=[jax.ShapeDtypeStruct(*out) for out in outs],
         scratch_shapes=scratch,
@@ -240,53 +273,30 @@
     )(*operands)
 
 
-def in_order(workers):
-    return list(range(workers - 1, 0, -1))
-
-
-def out_order(workers):
-    return list(range(workers - 1, 0, -1))
-
-
 def step(mono_ham, polymer_members, polymer_coupling):
     workers = lax.axis_size("wrk")
     groups = lax.axis_size("grp")
     n = mono_ham.shape[-1]
     tall, wide = n + PAD, n // 2
     packed, own = call(pack_kernel, (mono_ham,), [((1, tall, wide), BF16), ((n, n), BF16)], flops=1000)
-    mates = {}
-    for k in in_order(workers):
-        mates[k] = from_behind(packed, "wrk", -k)
-    following = []
-    for k in range(workers):
-        following.append(from_behind(mates[k] if k else packed, "grp", -1))
-    n_rows = 4 * workers + 2
+    candidates = gather(packed)
     frame, known, rows = call(
         functools.partial(early_kernel, workers=workers, groups=groups),
         (polymer_members, own, polymer_coupling),
-        [((3 * n, 3 * n), BF16), ((3 * n, 3 * n), F32), ((n_rows, wide), F32)],
+        [((3 * n, 3 * n), BF16), ((3 * n, 3 * n), F32), ((3 * workers - 1, wide), F32)],
         flops=2 * 18 * n**3,
-        spaces={0: pltpu.SMEM},
     )
-    going, frame, crossed = call(
+    targets = everyone(workers)
+    *sent, frame, crossed = call(
         functools.partial(main_kernel, workers=workers),
-        [mates[k] for k in range(1, workers)] + following + [frame, known, rows],
-        [((2, tall, wide), BF16), ((3 * n, 3 * n), BF16), ((2, n, n), BF16)],
+        candidates + [frame, known, rows],
+        [((1, tall, wide), BF16)] * len(targets) + [((3 * n, 3 * n), BF16), ((2, n, n), BF16)],
         flops=2 * 45 * n**3,
         scratch=[pltpu.VMEM((3 * n, 3 * n), BF16)],
     )
-    back = from_behind(going, "grp", 1)
+    received = give_back(dict(zip(targets, sent)))
     mine, delta = call(own_kernel, (own, frame, crossed), [((n, n), F32)] * 2, flops=2 * 10 * n**3)
-    sums = call(
-        functools.partial(collect_kernel, workers=workers),
-        (back, going, rows),
-        [((1, tall, wide), BF16)] * workers,
-        flops=1000,
-    )
-    received = []
-    for k in out_order(workers):
-        received.append(from_behind(sums[k], "wrk", -k))
-    (density,) = call(finish_kernel, [sums[0]] + received + [mine, delta], [((1, n, n), F32)], flops=1000)
+    (density,) = call(finish_kernel, received + [mine, delta], [((1, n, n), F32)], flops=1000)
     return density
 
 

time: 34.4 us -> 31.9 us (0.927)
  waiting for transfers between devices: 9.39 us -> 4.74 us
  starting transfers between devices: 16.3 us -> 19.1 us
  Pallas kernels: 5.83 us -> 5.23 us
    ppermute x11 -> x14, waiting for transfers between devices: 9.39 us -> 4.74 us  [the longest x7 3.61 us: to_mate(): return lax.ppermute(block, ('grp', 'wrk'), list(pairs(distance, k)))]
    ppermute x11 -> x14, starting transfers between devices: 16.3 us -> 19.1 us  [the longest x7 11.8 us: from_mate(): lax.ppermute(block, ('grp', 'wrk'), [(there, here) for here, there in pai...]
    pallas_call x6, Pallas kernels: 5.83 us -> 5.23 us  [call(): pl.pallas_call(kernel, in_specs=[vmem] * len(operands), out_specs=[vmem]...]
  transfers between devices with their start and end apart: 11 -> 14, of which waited for: 5 -> 4; matrix products, arithmetic and copies ran while one was open for 0% -> 0% of each run, Pallas kernels for 7% -> 6%
where the time goes in v1:
time: 31.9 us; the launch traced here: 31.7 us
  starting transfers between devices  19.1 us (60%)
  Pallas kernels  5.23 us (16%)
  waiting for transfers between devices  4.74 us (15%)
  local copies, waits for them, and re-layouts  2.55 us (8%)
    ppermute x7, starting transfers between devices, from_mate(): lax.ppermute(block, ('grp', 'wrk'), [(there, here) for here, there in pai...  11.8 us
    ppermute x7, starting transfers between devices, to_mate(): return lax.ppermute(block, ('grp', 'wrk'), list(pairs(distance, k)))  7.24 us
    pallas_call x6, Pallas kernels, call(): pl.pallas_call(kernel, in_specs=[vmem] * len(operands), out_specs=[vmem]...  5.23 us
    ppermute x7, waiting for transfers between devices, to_mate(): return lax.ppermute(block, ('grp', 'wrk'), list(pairs(distance, k)))  3.61 us
    unnamed x6, local copies, waits for them, and re-layouts  2.55 us
    ppermute x7, waiting for transfers between devices, from_mate(): lax.ppermute(block, ('grp', 'wrk'), [(there, here) for here, there in pai...  1.13 us
  transfers between devices with their start and end apart: 14, of which 4 were waited for; matrix products, arithmetic and copies ran while one was open for 0% of the time, Pallas kernels for 6%

profile of v1, /device:TPU:0, one launch (start us, length us, event | category | flops | bytes accessed | tf_op | source)
XLA Modules:
  0.0 31.7 jit_solution(12957437367785823871)
XLA Ops:
  0.0 0.0 copy-start
  0.0 0.9 %copy-done = bf16[1,256,256]{2,1,0:T(8,128)(2,1)S(1)} copy-done((bf16[1,256,256]{2,1,0:T(8,128)(2,1)S(1)}, bf16[1,256,256]{2,1,0:T(8,128)(2,1)}, u32[]{:S(2)}) %copy-start) | copy-done | bytes 131096
  0.9 0.1 shard_map.37
  1.0 4.1 %collective-permute-start.1 = (bf16[1,264,128]{2,1,0:T(8,128)(2,1)S(1)}, bf16[1,264,128]{2,1,0:T(8,128)(2,1)S(1)}, u32[]{:S(2)}, u32[]{:S(2)}) collective-permute-start(bf16[1,264,128]{2,1,0:T(8,128)(2,1)S(1)} %get-tuple-element.21), channel_id=1, source_target_pairs={{2,0},{3,1},{0,2},{1,3},{6,4},{7,5},{4,6},{5,7},{10,8},{11,9},{8,1... | collective-permute-start | bytes 202760 | tf_op jit(solution)/shard_map/ppermute | solution.py:29
  5.1 2.6 %collective-permute-start.4 = (bf16[1,264,128]{2,1,0:T(8,128)(2,1)S(1)}, bf16[1,264,128]{2,1,0:T(8,128)(2,1)S(1)}, u32[]{:S(2)}, u32[]{:S(2)}) collective-permute-start(bf16[1,264,128]{2,1,0:T(8,128)(2,1)S(1)} %get-tuple-element.21), channel_id=1, source_target_pairs={{5,0},{4,1},{7,2},{6,3},{9,4},{8,5},{11,6},{10,7},{13,8},{12,9},{1... | collective-permute-start | bytes 202760 | tf_op jit(solution)/shard_map/ppermute | solution.py:29
  7.7 1.1 %collective-permute-start.3 = (bf16[1,264,128]{2,1,0:T(8,128)(2,1)S(1)}, bf16[1,264,128]{2,1,0:T(8,128)(2,1)S(1)}, u32[]{:S(2)}, u32[]{:S(2)}) collective-permute-start(bf16[1,264,128]{2,1,0:T(8,128)(2,1)S(1)} %get-tuple-element.21), channel_id=1, source_target_pairs={{4,0},{5,1},{6,2},{7,3},{8,4},{9,5},{10,6},{11,7},{12,8},{13,9},{1... | collective-permute-start | bytes 202760 | tf_op jit(solution)/shard_map/ppermute | solution.py:29
  8.8 0.4 %collective-permute-start = (bf16[1,264,128]{2,1,0:T(8,128)(2,1)S(1)}, bf16[1,264,128]{2,1,0:T(8,128)(2,1)S(1)}, u32[]{:S(2)}, u32[]{:S(2)}) collective-permute-start(bf16[1,264,128]{2,1,0:T(8,128)(2,1)S(1)} %get-tuple-element.21), channel_id=1, source_target_pairs={{1,0},{0,1},{3,2},{2,3},{5,4},{4,5},{7,6},{6,7},{9,8},{8,9},{11,10... | collective-permute-start | bytes 202760 | tf_op jit(solution)/shard_map/ppermute | solution.py:29
  9.3 0.0 collective-permute-done.1.refs_1_
  9.3 1.2 %collective-permute-start.6 = (bf16[1,264,128]{2,1,0:T(8,128)(2,1)S(1)}, bf16[1,264,128]{2,1,0:T(8,128)(2,1)S(1)}, u32[]{:S(2)}, u32[]{:S(2)}) collective-permute-start(bf16[1,264,128]{2,1,0:T(8,128)(2,1)S(1)} %collective-permute-done.1.refs_1_), channel_id=1, source_target_pairs={{5,0},{4,1},{7,2},{6,3},{9,4},{8,5},{11,6},{10,7},{13,8},{12,9},{1... | collective-permute-start | bytes 202760 | tf_op jit(solution)/shard_map/ppermute | solution.py:29
  10.5 1.7 %collective-permute-start.5 = (bf16[1,264,128]{2,1,0:T(8,128)(2,1)S(1)}, bf16[1,264,128]{2,1,0:T(8,128)(2,1)S(1)}, u32[]{:S(2)}, u32[]{:S(2)}) collective-permute-start(bf16[1,264,128]{2,1,0:T(8,128)(2,1)S(1)} %collective-permute-done.1.refs_1_), channel_id=1, source_target_pairs={{4,0},{5,1},{6,2},{7,3},{8,4},{9,5},{10,6},{11,7},{12,8},{13,9},{1... | collective-permute-start | bytes 202760 | tf_op jit(solution)/shard_map/ppermute | solution.py:29
  12.2 0.0 collective-permute-done.4.refs_4_
  12.2 0.6 %collective-permute-start.2 = (bf16[1,264,128]{2,1,0:T(8,128)(2,1)S(1)}, bf16[1,264,128]{2,1,0:T(8,128)(2,1)S(1)}, u32[]{:S(2)}, u32[]{:S(2)}) collective-permute-start(bf16[1,264,128]{2,1,0:T(8,128)(2,1)S(1)} %collective-permute-done.1.refs_1_), channel_id=1, source_target_pairs={{1,0},{0,1},{3,2},{2,3},{5,4},{4,5},{7,6},{6,7},{9,8},{8,9},{11,10... | collective-permute-start | bytes 202760 | tf_op jit(solution)/shard_map/ppermute | solution.py:29
  12.8 0.0 copy-start.1
  12.8 1.0 %copy-done.1 = bf16[1,3,256,256]{3,2,1,0:T(8,128)(2,1)S(1)} copy-done((bf16[1,3,256,256]{3,2,1,0:T(8,128)(2,1)S(1)}, bf16[1,3,256,256]{3,2,1,0:T(8,128)(2,1)}, u32[]{:S(2)}) %copy-start.1) | copy-done | bytes 393240
  13.8 0.0 copy-start.2
  13.8 0.7 %copy-done.2 = s32[1,3]{1,0:T(1,128)S(1)} copy-done((s32[1,3]{1,0:T(1,128)S(1)}, s32[1,3]{1,0:T(1,128)}, u32[]{:S(2)}) %copy-start.2) | copy-done | bytes 36
  14.5 0.8 %shard_map.38 = (bf16[768,768]{1,0:T(8,128)(2,1)S(1)}, f32[768,768]{1,0:T(8,128)S(1)}, f32[11,128]{1,0:T(8,128)S(1)}) custom-call(s32[1,3]{1,0:T(1,128)S(1)} %copy-done.2, bf16[256,256]{1,0:T(8,128)(2,1)S(1)} %get-tuple-element.22.own_ref.own, bf16[1,3,256,256]{3,2,1,0:T(8,128)(2,1)S(1)} %copy-done.1), custom_call_target="tpu_custom_call" | custom-call | flops 603979776 | tf_op jit(solution)/shard_map/pallas_call | solution.py:265
  15.3 0.0 collective-permute-done.3.refs_3_
  15.3 0.0 collective-permute-done.refs_0_
  15.3 0.0 collective-permute-done.6.refs_6_
  15.3 0.0 collective-permute-done.5.refs_5_
  15.3 1.1 %collective-permute-done.2.refs_2_ = bf16[1,264,128]{2,1,0:T(8,128)(2,1)S(1)} collective-permute-done((bf16[1,264,128]{2,1,0:T(8,128)(2,1)S(1)}, bf16[1,264,128]{2,1,0:T(8,128)(2,1)S(1)}, u32[]{:S(2)}, u32[]{:S(2)}) %collective-permute-start.2) | collective-permute-done | bytes 67616 | tf_op jit(solution)/shard_map/ppermute | solution.py:29
  16.5 2.4 %shard_map.39 = (bf16[1,264,128]{2,1,0:T(8,128)(2,1)S(1)}, bf16[1,264,128]{2,1,0:T(8,128)(2,1)S(1)}, bf16[1,264,128]{2,1,0:T(8,128)(2,1)S(1)}, bf16[1,264,128]{2...) custom-call(bf16[1,264,128]{2,1,0:T(8,128)(2,1)S(1)} %collective-per, ...), custom_call_target="tpu_custom_call" | custom-call | flops 1509949440 | tf_op jit(solution)/shard_map/pallas_call | solution.py:265
  18.9 0.1 collective-permute-start.10
  19.0 1.1 %collective-permute-start.11 = (bf16[1,264,128]{2,1,0:T(8,128)(2,1)S(1)}, bf16[1,264,128]{2,1,0:T(8,128)(2,1)S(1)}, u32[]{:S(2)}, u32[]{:S(2)}) collective-permute-start(bf16[1,264,128]{2,1,0:T(8,128)(2,1)S(1)} %get-tuple-element.30), channel_id=1, source_target_pairs={{0,4},{1,5},{2,6},{3,7},{4,8},{5,9},{6,10},{7,11},{8,12},{9,13},{1... | collective-permute-start | bytes 202760 | tf_op jit(solution)/shard_map/ppermute | solution.py:33
  20.0 0.9 %collective-permute-start.12 = (bf16[1,264,128]{2,1,0:T(8,128)(2,1)S(1)}, bf16[1,264,128]{2,1,0:T(8,128)(2,1)S(1)}, u32[]{:S(2)}, u32[]{:S(2)}) collective-permute-start(bf16[1,264,128]{2,1,0:T(8,128)(2,1)S(1)} %get-tuple-element.31), channel_id=1, source_target_pairs={{0,1},{1,0},{2,3},{3,2},{4,5},{5,4},{6,7},{7,6},{8,9},{9,8},{10,11... | collective-permute-start | bytes 202760 | tf_op jit(solution)/shard_map/ppermute | solution.py:33
  21.0 0.0 collective-permute-start.7
  21.0 1.9 %collective-permute-start.8 = (bf16[1,264,128]{2,1,0:T(8,128)(2,1)S(1)}, bf16[1,264,128]{2,1,0:T(8,128)(2,1)S(1)}, u32[]{:S(2)}, u32[]{:S(2)}) collective-permute-start(bf16[1,264,128]{2,1,0:T(8,128)(2,1)S(1)} %get-tuple-element.27), channel_id=1, source_target_pairs={{0,5},{1,4},{2,7},{3,6},{4,9},{5,8},{6,11},{7,10},{8,13},{9,12},{1... | collective-permute-start | bytes 202760 | tf_op jit(solution)/shard_map/ppermute | solution.py:33
  22.8 1.6 %collective-permute-done.10.refs_0_ = bf16[1,264,128]{2,1,0:T(8,128)(2,1)S(1)} collective-permute-done((bf16[1,264,128]{2,1,0:T(8,128)(2,1)S(1)}, bf16[1,264,128]{2,1,0:T(8,128)(2,1)S(1)}, u32[]{:S(2)}, u32[]{:S(2)}) %collective-permute-start.10) | collective-permute-done | bytes 67616 | tf_op jit(solution)/shard_map/ppermute | solution.py:33
  24.5 0.7 %collective-permute-start.9 = (bf16[1,264,128]{2,1,0:T(8,128)(2,1)S(1)}, bf16[1,264,128]{2,1,0:T(8,128)(2,1)S(1)}, u32[]{:S(2)}, u32[]{:S(2)}) collective-permute-start(bf16[1,264,128]{2,1,0:T(8,128)(2,1)S(1)} %get-tuple-element.28), channel_id=1, source_target_pairs={{0,1},{1,0},{2,3},{3,2},{4,5},{5,4},{6,7},{7,6},{8,9},{9,8},{10,11... | collective-permute-start | bytes 202760 | tf_op jit(solution)/shard_map/ppermute | solution.py:33
  25.2 0.0 collective-permute-done.11.refs_1_
  25.2 0.0 collective-permute-done.12.refs_2_
  25.2 2.6 %collective-permute-start.13 = (bf16[1,264,128]{2,1,0:T(8,128)(2,1)S(1)}, bf16[1,264,128]{2,1,0:T(8,128)(2,1)S(1)}, u32[]{:S(2)}, u32[]{:S(2)}) collective-permute-start(bf16[1,264,128]{2,1,0:T(8,128)(2,1)S(1)} %shard_map.40), channel_id=1, source_target_pairs={{0,2},{1,3},{2,0},{3,1},{4,6},{5,7},{6,4},{7,5},{8,10},{9,11},{10,... | collective-permute-start | bytes 202760 | tf_op jit(solution)/shard_map/ppermute | solution.py:33
  27.8 1.0 %shard_map.41 = (f32[256,256]{1,0:T(8,128)S(1)}, f32[256,256]{1,0:T(8,128)S(1)}) custom-call(bf16[256,256]{1,0:T(8,128)(2,1)S(1)} %get-tuple-element.22.own_ref.own, bf16[768,768]{1,0:T(8,128)(2,1)S(1)} %get-tuple-element.33.frame, bf16[2,256,256]{2,1,0:T(8,128)(2,1)S(1)} %get-tuple-element.34.crossed), custom_call_target="tpu_custom_call" | custom-call | flops 335544320 | tf_op jit(solution)/shard_map/pallas_call | solution.py:265
  28.9 0.0 collective-permute-done.7.refs_0_
  28.9 0.0 collective-permute-done.8.refs_1_
  28.9 0.2 collective-permute-done.9.refs_2_
  29.1 1.8 %collective-permute-done.13.refs_3_ = bf16[1,264,128]{2,1,0:T(8,128)(2,1)S(1)} collective-permute-done((bf16[1,264,128]{2,1,0:T(8,128)(2,1)S(1)}, bf16[1,264,128]{2,1,0:T(8,128)(2,1)S(1)}, u32[]{:S(2)}, u32[]{:S(2)}) %collective-permute-start.13) | collective-permute-done | bytes 67616 | tf_op jit(solution)/shard_map/ppermute | solution.py:33
  30.9 0.8 %shard_map.42 = f32[1,256,256]{2,1,0:T(8,128)} custom-call(bf16[1,264,128]{2,1,0:T(8,128)(2,1)S(1)} %collective-permute-done.7.refs_0_, bf16[1,264,128]{2,1,0:T(8,128)(2,1)S(1)} %collective-permute-done.8.refs_1_, bf16[1,264,128]{2,1,0:T(8,128)(2,1)S(1)} %collective-permute-done.9.refs_2_, bf16[1,264,128]{2,1,0:T(8,128)(2,1)S(1)} %collective-permute-done.13.refs_3_, ...), custom_call_target="tpu_custom_call" | custom-call | flops 1000 | tf_op jit(solution)/shard_map/pallas_call | solution.py:265
  (1 shorter events, 0.0 us)
Async XLA Ops:
  0.0 0.9 %copy-start = (bf16[1,256,256]{2,1,0:T(8,128)(2,1)S(1)}, bf16[1,256,256]{2,1,0:T(8,128)(2,1)}, u32[]{:S(2)}) copy-start(bf16[1,256,256]{2,1,0:T(8,128)(2,1)} %ham.1) | copy-start | bytes 393220
  1.0 8.3 %collective-permute-start.1 = (bf16[1,264,128]{2,1,0:T(8,128)(2,1)S(1)}, bf16[1,264,128]{2,1,0:T(8,128)(2,1)S(1)}, u32[]{:S(2)}, u32[]{:S(2)}) collective-permute-start(bf16[1,264,128]{2,1,0:T(8,128)(2,1)S(1)} %get-tuple-element.21), channel_id=1, source_target_pairs={{2,0},{3,1},{0,2},{1,3},{6,4},{7,5},{4,6},{5,7},{10,8},{11,9},{8,1... | collective-permute-start | bytes 202760 | tf_op jit(solution)/shard_map/ppermute | solution.py:29
  5.1 7.1 %collective-permute-start.4 = (bf16[1,264,128]{2,1,0:T(8,128)(2,1)S(1)}, bf16[1,264,128]{2,1,0:T(8,128)(2,1)S(1)}, u32[]{:S(2)}, u32[]{:S(2)}) collective-permute-start(bf16[1,264,128]{2,1,0:T(8,128)(2,1)S(1)} %get-tuple-element.21), channel_id=1, source_target_pairs={{5,0},{4,1},{7,2},{6,3},{9,4},{8,5},{11,6},{10,7},{13,8},{12,9},{1... | collective-permute-start | bytes 202760 | tf_op jit(solution)/shard_map/ppermute | solution.py:29
  7.7 7.6 %collective-permute-start.3 = (bf16[1,264,128]{2,1,0:T(8,128)(2,1)S(1)}, bf16[1,264,128]{2,1,0:T(8,128)(2,1)S(1)}, u32[]{:S(2)}, u32[]{:S(2)}) collective-permute-start(bf16[1,264,128]{2,1,0:T(8,128)(2,1)S(1)} %get-tuple-element.21), channel_id=1, source_target_pairs={{4,0},{5,1},{6,2},{7,3},{8,4},{9,5},{10,6},{11,7},{12,8},{13,9},{1... | collective-permute-start | bytes 202760 | tf_op jit(solution)/shard_map/ppermute | solution.py:29
  8.8 6.5 %collective-permute-start = (bf16[1,264,128]{2,1,0:T(8,128)(2,1)S(1)}, bf16[1,264,128]{2,1,0:T(8,128)(2,1)S(1)}, u32[]{:S(2)}, u32[]{:S(2)}) collective-permute-start(bf16[1,264,128]{2,1,0:T(8,128)(2,1)S(1)} %get-tuple-element.21), channel_id=1, source_target_pairs={{1,0},{0,1},{3,2},{2,3},{5,4},{4,5},{7,6},{6,7},{9,8},{8,9},{11,10... | collective-permute-start | bytes 202760 | tf_op jit(solution)/shard_map/ppermute | solution.py:29
  9.3 6.0 %collective-permute-start.6 = (bf16[1,264,128]{2,1,0:T(8,128)(2,1)S(1)}, bf16[1,264,128]{2,1,0:T(8,128)(2,1)S(1)}, u32[]{:S(2)}, u32[]{:S(2)}) collective-permute-start(bf16[1,264,128]{2,1,0:T(8,128)(2,1)S(1)} %collective-permute-done.1.refs_1_), channel_id=1, source_target_pairs={{5,0},{4,1},{7,2},{6,3},{9,4},{8,5},{11,6},{10,7},{13,8},{12,9},{1... | collective-permute-start | bytes 202760 | tf_op jit(solution)/shard_map/ppermute | solution.py:29
  10.5 4.9 %collective-permute-start.5 = (bf16[1,264,128]{2,1,0:T(8,128)(2,1)S(1)}, bf16[1,264,128]{2,1,0:T(8,128)(2,1)S(1)}, u32[]{:S(2)}, u32[]{:S(2)}) collective-permute-start(bf16[1,264,128]{2,1,0:T(8,128)(2,1)S(1)} %collective-permute-done.1.refs_1_), channel_id=1, source_target_pairs={{4,0},{5,1},{6,2},{7,3},{8,4},{9,5},{10,6},{11,7},{12,8},{13,9},{1... | collective-permute-start | bytes 202760 | tf_op jit(solution)/shard_map/ppermute | solution.py:29
  12.2 4.3 %collective-permute-start.2 = (bf16[1,264,128]{2,1,0:T(8,128)(2,1)S(1)}, bf16[1,264,128]{2,1,0:T(8,128)(2,1)S(1)}, u32[]{:S(2)}, u32[]{:S(2)}) collective-permute-start(bf16[1,264,128]{2,1,0:T(8,128)(2,1)S(1)} %collective-permute-done.1.refs_1_), channel_id=1, source_target_pairs={{1,0},{0,1},{3,2},{2,3},{5,4},{4,5},{7,6},{6,7},{9,8},{8,9},{11,10... | collective-permute-start | bytes 202760 | tf_op jit(solution)/shard_map/ppermute | solution.py:29
  12.8 1.0 %copy-start.1 = (bf16[1,3,256,256]{3,2,1,0:T(8,128)(2,1)S(1)}, bf16[1,3,256,256]{3,2,1,0:T(8,128)(2,1)}, u32[]{:S(2)}) copy-start(bf16[1,3,256,256]{3,2,1,0:T(8,128)(2,1)} %coupling.1) | copy-start | bytes 1179652
  13.8 0.7 %copy-start.2 = (s32[1,3]{1,0:T(1,128)S(1)}, s32[1,3]{1,0:T(1,128)}, u32[]{:S(2)}) copy-start(s32[1,3]{1,0:T(1,128)} %members.1) | copy-start | bytes 40
  18.9 5.6 %collective-permute-start.10 = (bf16[1,264,128]{2,1,0:T(8,128)(2,1)S(1)}, bf16[1,264,128]{2,1,0:T(8,128)(2,1)S(1)}, u32[]{:S(2)}, u32[]{:S(2)}) collective-permute-start(bf16[1,264,128]{2,1,0:T(8,128)(2,1)S(1)} %get-tuple-element.29), channel_id=1, source_target_pairs={{0,5},{1,4},{2,7},{3,6},{4,9},{5,8},{6,11},{7,10},{8,13},{9,12},{1... | collective-permute-start | bytes 202760 | tf_op jit(solution)/shard_map/ppermute | solution.py:33
  19.0 6.2 %collective-permute-start.11 = (bf16[1,264,128]{2,1,0:T(8,128)(2,1)S(1)}, bf16[1,264,128]{2,1,0:T(8,128)(2,1)S(1)}, u32[]{:S(2)}, u32[]{:S(2)}) collective-permute-start(bf16[1,264,128]{2,1,0:T(8,128)(2,1)S(1)} %get-tuple-element.30), channel_id=1, source_target_pairs={{0,4},{1,5},{2,6},{3,7},{4,8},{5,9},{6,10},{7,11},{8,12},{9,13},{1... | collective-permute-start | bytes 202760 | tf_op jit(solution)/shard_map/ppermute | solution.py:33
  20.0 5.2 %collective-permute-start.12 = (bf16[1,264,128]{2,1,0:T(8,128)(2,1)S(1)}, bf16[1,264,128]{2,1,0:T(8,128)(2,1)S(1)}, u32[]{:S(2)}, u32[]{:S(2)}) collective-permute-start(bf16[1,264,128]{2,1,0:T(8,128)(2,1)S(1)} %get-tuple-element.31), channel_id=1, source_target_pairs={{0,1},{1,0},{2,3},{3,2},{4,5},{5,4},{6,7},{7,6},{8,9},{9,8},{10,11... | collective-permute-start | bytes 202760 | tf_op jit(solution)/shard_map/ppermute | solution.py:33
  21.0 7.9 %collective-permute-start.7 = (bf16[1,264,128]{2,1,0:T(8,128)(2,1)S(1)}, bf16[1,264,128]{2,1,0:T(8,128)(2,1)S(1)}, u32[]{:S(2)}, u32[]{:S(2)}) collective-permute-start(bf16[1,264,128]{2,1,0:T(8,128)(2,1)S(1)} %get-tuple-element.26), channel_id=1, source_target_pairs={{0,4},{1,5},{2,6},{3,7},{4,8},{5,9},{6,10},{7,11},{8,12},{9,13},{1... | collective-permute-start | bytes 202760 | tf_op jit(solution)/shard_map/ppermute | solution.py:33
  21.0 7.9 %collective-permute-start.8 = (bf16[1,264,128]{2,1,0:T(8,128)(2,1)S(1)}, bf16[1,264,128]{2,1,0:T(8,128)(2,1)S(1)}, u32[]{:S(2)}, u32[]{:S(2)}) collective-permute-start(bf16[1,264,128]{2,1,0:T(8,128)(2,1)S(1)} %get-tuple-element.27), channel_id=1, source_target_pairs={{0,5},{1,4},{2,7},{3,6},{4,9},{5,8},{6,11},{7,10},{8,13},{9,12},{1... | collective-permute-start | bytes 202760 | tf_op jit(solution)/shard_map/ppermute | solution.py:33
  24.5 4.7 %collective-permute-start.9 = (bf16[1,264,128]{2,1,0:T(8,128)(2,1)S(1)}, bf16[1,264,128]{2,1,0:T(8,128)(2,1)S(1)}, u32[]{:S(2)}, u32[]{:S(2)}) collective-permute-start(bf16[1,264,128]{2,1,0:T(8,128)(2,1)S(1)} %get-tuple-element.28), channel_id=1, source_target_pairs={{0,1},{1,0},{2,3},{3,2},{4,5},{5,4},{6,7},{7,6},{8,9},{9,8},{10,11... | collective-permute-start | bytes 202760 | tf_op jit(solution)/shard_map/ppermute | solution.py:33
  25.2 5.6 %collective-permute-start.13 = (bf16[1,264,128]{2,1,0:T(8,128)(2,1)S(1)}, bf16[1,264,128]{2,1,0:T(8,128)(2,1)S(1)}, u32[]{:S(2)}, u32[]{:S(2)}) collective-permute-start(bf16[1,264,128]{2,1,0:T(8,128)(2,1)S(1)} %shard_map.40), channel_id=1, source_target_pairs={{0,2},{1,3},{2,0},{3,1},{4,6},{5,7},{6,4},{7,5},{8,10},{9,11},{10,... | collective-permute-start | bytes 202760 | tf_op jit(solution)/shard_map/ppermute | solution.py:33

commit v2 on v1

--- a/solution.py
+++ b/solution.py
@@ -39,7 +39,7 @@
 
 def gather_plan(workers):
     if workers == 4:
-        return [(0, 2, None), (1, 1, None), (0, 1, None), (1, 0, None), (0, 1, 2), (1, 1, 2), (1, 0, 2)]
+        return [(0, 2, None), (0, 1, None), (1, 1, None), (1, 0, None), (0, 1, 2), (1, 0, 2), (1, 1, 2)]
     return [(distance, k, None) for distance, k in everyone(workers)]
 
 
@@ -121,8 +121,15 @@
     own[...] = block.astype(BF16)
 
 
-def early_kernel(members, own_ref, coupling, frame, known, rows, *, workers, groups):
+def early_kernel(
+    members_hbm, coupling_hbm, own_ref, frame, known, rows, members, coupling, arrived, *, workers, groups
+):
     n = own_ref.shape[-1]
+    listing = pltpu.make_async_copy(members_hbm, members, arrived.at[0])
+    fetch = pltpu.make_async_copy(coupling_hbm, coupling, arrived.at[1])
+    listing.start()
+    fetch.start()
+    listing.wait()
     group = lax.axis_index("grp")
     slot = lax.axis_index("wrk")
     following = lax.rem(group + 1, groups)
@@ -144,6 +151,7 @@
             put(hit(member, following, mate(slot, k, workers)))
     own = own_ref[...]
     third = jnp.where(last >= 0, 1.0, 0.0)
+    fetch.wait()
     c01 = -0.35 * coupling[0, 0].astype(F32)
     c02 = -0.35 * coupling[0, 1].astype(F32) * third
     c12 = -0.35 * coupling[0, 2].astype(F32) * third
@@ -203,21 +211,28 @@
         low[part(i), part(j)] = value.astype(BF16)
         if i < j:
             low[part(j), part(i)] = value.T.astype(BF16)
-    for j in range(3):
-        product = dot(rectangle(blocks, range(j + 1), range(3)), low[:, part(j)])
-        for i in range(j + 1):
-            value = 3.0 * square[i, j] - 2.0 * product[part(i)]
-            frame[part(i), part(j)] = value.astype(BF16)
-            if i < j:
-                frame[part(j), part(i)] = value.T.astype(BF16)
-    square = {}
-    for j in (1, 2):
-        product = dot(frame[: (j + 1) * n, :], frame[:, part(j)])
-        for i in range(j + 1):
-            square[i, j] = product[part(i)]
-            low[part(i), part(j)] = square[i, j].astype(BF16)
-            if i == 1 and j == 2:
-                low[part(j), part(i)] = square[i, j].T.astype(BF16)
+    products = {}
+
+    def multiply(table, down, across):
+        product = dot(rectangle(table, down, range(3)), low[:, across[0] * n : (across[-1] + 1) * n])
+        for a, i in enumerate(down):
+            for b, j in enumerate(across):
+                products[i, j] = product[part(a), part(b)]
+
+    multiply(blocks, (0, 1), (1, 2))
+    multiply(blocks, (2,), (2,))
+    multiply(blocks, (0,), (0,))
+    for i, j in ((0, 2), (1, 2), (2, 2), (0, 1), (1, 1), (0, 0)):
+        value = 3.0 * square[i, j] - 2.0 * products[i, j]
+        frame[part(i), part(j)] = value.astype(BF16)
+        if i < j:
+            frame[part(j), part(i)] = value.T.astype(BF16)
+    product = dot(frame[: 2 * n, :], frame[:, n:])
+    square = {(i, j): product[part(i), part(j - 1)] for i in (0, 1) for j in (1, 2)}
+    square[2, 2] = dot(frame[2 * n :, :], frame[:, 2 * n :])
+    for (i, j), value in square.items():
+        low[part(i), part(j)] = value.astype(BF16)
+    low[part(2), part(1)] = square[1, 2].T.astype(BF16)
     crossed[0] = square[0, 1].T.astype(BF16)
     crossed[1] = square[0, 2].T.astype(BF16)
     pieces = []
@@ -260,11 +275,15 @@
         out[0, down, across] = mine[down, across] + count * delta[down, across] + value
 
 
-def call(kernel, operands, outs, flops=0, scratch=(), limit=24):
+def in_hbm(array):
+    return pltpu.with_memory_space_constraint(array, pltpu.HBM)
+
+
+def call(kernel, operands, outs, flops=0, scratch=(), distant=0, limit=24):
     vmem = pl.BlockSpec(memory_space=pltpu.VMEM)
     return pl.pallas_call(
         kernel,
-        in_specs=[vmem] * len(operands),
+        in_specs=[pl.BlockSpec(memory_space=pltpu.HBM)] * distant + [vmem] * (len(operands) - distant),
         out_specs=[vmem] * len(outs),
         out_shape=[jax.ShapeDtypeStruct(*out) for out in outs],
         scratch_shapes=scratch,
@@ -282,9 +301,15 @@
     candidates = gather(packed)
     frame, known, rows = call(
         functools.partial(early_kernel, workers=workers, groups=groups),
-        (polymer_members, own, polymer_coupling),
+        (in_hbm(polymer_members), in_hbm(polymer_coupling), own),
         [((3 * n, 3 * n), BF16), ((3 * n, 3 * n), F32), ((3 * workers - 1, wide), F32)],
         flops=2 * 18 * n**3,
+        distant=2,
+        scratch=[
+            pltpu.VMEM(polymer_members.shape, jnp.int32),
+            pltpu.VMEM(polymer_coupling.shape, BF16),
+            pltpu.SemaphoreType.DMA((2,)),
+        ],
     )
     targets = everyone(workers)
     *sent, frame, crossed = call(

time: 31.9 us -> 31.6 us (level)
  local copies, waits for them, and re-layouts: 2.55 us -> 0.9 us
  Pallas kernels: 5.23 us -> 6.04 us
  waiting for transfers between devices: 4.74 us -> 5.45 us
    unnamed x6 -> x2, local copies, waits for them, and re-layouts: 2.55 us -> 0.9 us
    pallas_call x6, Pallas kernels: 5.23 us -> 6.04 us  [call(): pl.pallas_call(kernel, in_specs=[pl.BlockSpec(memory_space=pltpu.HBM)] *...]
    ppermute x7, waiting for transfers between devices: 1.13 us -> 1.75 us  [from_mate(): lax.ppermute(block, ('grp', 'wrk'), [(there, here) for here, there in pai...]
  transfers between devices with their start and end apart: 14 -> 14, of which waited for: 4 -> 4; matrix products, arithmetic and copies ran while one was open for 0% -> 0% of each run, Pallas kernels for 6% -> 9%
where the time goes in v2:
time: 31.6 us; the launch traced here: 31.5 us
  starting transfers between devices  19 us (60%)
  Pallas kernels  6.04 us (19%)
  waiting for transfers between devices  5.45 us (17%)
  local copies, waits for them, and re-layouts  0.9 us (3%)
    ppermute x7, starting transfers between devices, from_mate(): lax.ppermute(block, ('grp', 'wrk'), [(there, here) for here, there in pai...  11.8 us
    ppermute x7, starting transfers between devices, to_mate(): return lax.ppermute(block, ('grp', 'wrk'), list(pairs(distance, k)))  7.15 us
    pallas_call x6, Pallas kernels, call(): pl.pallas_call(kernel, in_specs=[pl.BlockSpec(memory_space=pltpu.HBM)] *...  6.04 us
    ppermute x7, waiting for transfers between devices, to_mate(): return lax.ppermute(block, ('grp', 'wrk'), list(pairs(distance, k)))  3.7 us
    ppermute x7, waiting for transfers between devices, from_mate(): lax.ppermute(block, ('grp', 'wrk'), [(there, here) for here, there in pai...  1.75 us
    unnamed x2, local copies, waits for them, and re-layouts  0.9 us
  transfers between devices with their start and end apart: 14, of which 4 were waited for; matrix products, arithmetic and copies ran while one was open for 0% of the time, Pallas kernels for 9%

profile of v2, /device:TPU:0, one launch (start us, length us, event | category | flops | bytes accessed | tf_op | source)
XLA Modules:
  0.0 31.5 jit_solution(17422756525518444757)
XLA Ops:
  0.0 0.0 copy-start
  0.0 0.9 %copy-done = bf16[1,256,256]{2,1,0:T(8,128)(2,1)S(1)} copy-done((bf16[1,256,256]{2,1,0:T(8,128)(2,1)S(1)}, bf16[1,256,256]{2,1,0:T(8,128)(2,1)}, u32[]{:S(2)}) %copy-start) | copy-done | bytes 131096
  0.9 0.1 shard_map.37
  1.0 4.1 %collective-permute-start.1 = (bf16[1,264,128]{2,1,0:T(8,128)(2,1)S(1)}, bf16[1,264,128]{2,1,0:T(8,128)(2,1)S(1)}, u32[]{:S(2)}, u32[]{:S(2)}) collective-permute-start(bf16[1,264,128]{2,1,0:T(8,128)(2,1)S(1)} %get-tuple-element.21), channel_id=1, source_target_pairs={{2,0},{3,1},{0,2},{1,3},{6,4},{7,5},{4,6},{5,7},{10,8},{11,9},{8,1... | collective-permute-start | bytes 202760 | tf_op jit(solution)/shard_map/ppermute | solution.py:29
  5.1 2.6 %collective-permute-start.4 = (bf16[1,264,128]{2,1,0:T(8,128)(2,1)S(1)}, bf16[1,264,128]{2,1,0:T(8,128)(2,1)S(1)}, u32[]{:S(2)}, u32[]{:S(2)}) collective-permute-start(bf16[1,264,128]{2,1,0:T(8,128)(2,1)S(1)} %get-tuple-element.21), channel_id=1, source_target_pairs={{5,0},{4,1},{7,2},{6,3},{9,4},{8,5},{11,6},{10,7},{13,8},{12,9},{1... | collective-permute-start | bytes 202760 | tf_op jit(solution)/shard_map/ppermute | solution.py:29
  7.7 1.1 %collective-permute-start.3 = (bf16[1,264,128]{2,1,0:T(8,128)(2,1)S(1)}, bf16[1,264,128]{2,1,0:T(8,128)(2,1)S(1)}, u32[]{:S(2)}, u32[]{:S(2)}) collective-permute-start(bf16[1,264,128]{2,1,0:T(8,128)(2,1)S(1)} %get-tuple-element.21), channel_id=1, source_target_pairs={{4,0},{5,1},{6,2},{7,3},{8,4},{9,5},{10,6},{11,7},{12,8},{13,9},{1... | collective-permute-start | bytes 202760 | tf_op jit(solution)/shard_map/ppermute | solution.py:29
  8.8 0.4 %collective-permute-start = (bf16[1,264,128]{2,1,0:T(8,128)(2,1)S(1)}, bf16[1,264,128]{2,1,0:T(8,128)(2,1)S(1)}, u32[]{:S(2)}, u32[]{:S(2)}) collective-permute-start(bf16[1,264,128]{2,1,0:T(8,128)(2,1)S(1)} %get-tuple-element.21), channel_id=1, source_target_pairs={{1,0},{0,1},{3,2},{2,3},{5,4},{4,5},{7,6},{6,7},{9,8},{8,9},{11,10... | collective-permute-start | bytes 202760 | tf_op jit(solution)/shard_map/ppermute | solution.py:29
  9.3 0.0 collective-permute-done.1.refs_1_
  9.3 1.2 %collective-permute-start.6 = (bf16[1,264,128]{2,1,0:T(8,128)(2,1)S(1)}, bf16[1,264,128]{2,1,0:T(8,128)(2,1)S(1)}, u32[]{:S(2)}, u32[]{:S(2)}) collective-permute-start(bf16[1,264,128]{2,1,0:T(8,128)(2,1)S(1)} %collective-permute-done.1.refs_1_), channel_id=1, source_target_pairs={{5,0},{4,1},{7,2},{6,3},{9,4},{8,5},{11,6},{10,7},{13,8},{12,9},{1... | collective-permute-start | bytes 202760 | tf_op jit(solution)/shard_map/ppermute | solution.py:29
  10.5 1.7 %collective-permute-start.5 = (bf16[1,264,128]{2,1,0:T(8,128)(2,1)S(1)}, bf16[1,264,128]{2,1,0:T(8,128)(2,1)S(1)}, u32[]{:S(2)}, u32[]{:S(2)}) collective-permute-start(bf16[1,264,128]{2,1,0:T(8,128)(2,1)S(1)} %collective-permute-done.1.refs_1_), channel_id=1, source_target_pairs={{4,0},{5,1},{6,2},{7,3},{8,4},{9,5},{10,6},{11,7},{12,8},{13,9},{1... | collective-permute-start | bytes 202760 | tf_op jit(solution)/shard_map/ppermute | solution.py:29
  12.2 0.0 collective-permute-done.4.refs_4_
  12.2 0.6 %collective-permute-start.2 = (bf16[1,264,128]{2,1,0:T(8,128)(2,1)S(1)}, bf16[1,264,128]{2,1,0:T(8,128)(2,1)S(1)}, u32[]{:S(2)}, u32[]{:S(2)}) collective-permute-start(bf16[1,264,128]{2,1,0:T(8,128)(2,1)S(1)} %collective-permute-done.1.refs_1_), channel_id=1, source_target_pairs={{1,0},{0,1},{3,2},{2,3},{5,4},{4,5},{7,6},{6,7},{9,8},{8,9},{11,10... | collective-permute-start | bytes 202760 | tf_op jit(solution)/shard_map/ppermute | solution.py:29
  12.8 1.9 %shard_map.38 = (bf16[768,768]{1,0:T(8,128)(2,1)S(1)}, f32[768,768]{1,0:T(8,128)S(1)}, f32[11,128]{1,0:T(8,128)S(1)}) custom-call(s32[1,3]{1,0:T(1,128)} %members_hbm.1, bf16[1,3,256,256]{3,2,1,0:T(8,128)(2,1)} %coupling_hbm.1, bf16[256,256]{1,0:T(8,128)(2,1)S(1)} %get-tuple-element.22.own_ref.own), custom_call_target="tpu_custom_call" | custom-call | flops 603979776 | tf_op jit(solution)/shard_map/pallas_call | solution.py:284
  14.7 0.0 collective-permute-done.3.refs_3_
  14.7 0.0 collective-permute-done.refs_0_
  14.7 0.0 collective-permute-done.6.refs_6_
  14.7 0.0 collective-permute-done.5.refs_5_
  14.7 1.7 %collective-permute-done.2.refs_2_ = bf16[1,264,128]{2,1,0:T(8,128)(2,1)S(1)} collective-permute-done((bf16[1,264,128]{2,1,0:T(8,128)(2,1)S(1)}, bf16[1,264,128]{2,1,0:T(8,128)(2,1)S(1)}, u32[]{:S(2)}, u32[]{:S(2)}) %collective-permute-start.2) | collective-permute-done | bytes 67616 | tf_op jit(solution)/shard_map/ppermute | solution.py:29
  16.5 2.2 %shard_map.39 = (bf16[1,264,128]{2,1,0:T(8,128)(2,1)S(1)}, bf16[1,264,128]{2,1,0:T(8,128)(2,1)S(1)}, bf16[1,264,128]{2,1,0:T(8,128)(2,1)S(1)}, bf16[1,264,128]{2...) custom-call(bf16[1,264,128]{2,1,0:T(8,128)(2,1)S(1)} %collective-per, ...), custom_call_target="tpu_custom_call" | custom-call | flops 1509949440 | tf_op jit(solution)/shard_map/pallas_call | solution.py:284
  18.7 0.1 collective-permute-start.10
  18.7 1.1 %collective-permute-start.11 = (bf16[1,264,128]{2,1,0:T(8,128)(2,1)S(1)}, bf16[1,264,128]{2,1,0:T(8,128)(2,1)S(1)}, u32[]{:S(2)}, u32[]{:S(2)}) collective-permute-start(bf16[1,264,128]{2,1,0:T(8,128)(2,1)S(1)} %get-tuple-element.30), channel_id=1, source_target_pairs={{0,4},{1,5},{2,6},{3,7},{4,8},{5,9},{6,10},{7,11},{8,12},{9,13},{1... | collective-permute-start | bytes 202760 | tf_op jit(solution)/shard_map/ppermute | solution.py:33
  19.8 0.9 %collective-permute-start.12 = (bf16[1,264,128]{2,1,0:T(8,128)(2,1)S(1)}, bf16[1,264,128]{2,1,0:T(8,128)(2,1)S(1)}, u32[]{:S(2)}, u32[]{:S(2)}) collective-permute-start(bf16[1,264,128]{2,1,0:T(8,128)(2,1)S(1)} %get-tuple-element.31), channel_id=1, source_target_pairs={{0,1},{1,0},{2,3},{3,2},{4,5},{5,4},{6,7},{7,6},{8,9},{9,8},{10,11... | collective-permute-start | bytes 202760 | tf_op jit(solution)/shard_map/ppermute | solution.py:33
  20.8 0.0 collective-permute-start.7
  20.8 1.9 %collective-permute-start.8 = (bf16[1,264,128]{2,1,0:T(8,128)(2,1)S(1)}, bf16[1,264,128]{2,1,0:T(8,128)(2,1)S(1)}, u32[]{:S(2)}, u32[]{:S(2)}) collective-permute-start(bf16[1,264,128]{2,1,0:T(8,128)(2,1)S(1)} %get-tuple-element.27), channel_id=1, source_target_pairs={{0,5},{1,4},{2,7},{3,6},{4,9},{5,8},{6,11},{7,10},{8,13},{9,12},{1... | collective-permute-start | bytes 202760 | tf_op jit(solution)/shard_map/ppermute | solution.py:33
  22.6 1.6 %collective-permute-done.10.refs_0_ = bf16[1,264,128]{2,1,0:T(8,128)(2,1)S(1)} collective-permute-done((bf16[1,264,128]{2,1,0:T(8,128)(2,1)S(1)}, bf16[1,264,128]{2,1,0:T(8,128)(2,1)S(1)}, u32[]{:S(2)}, u32[]{:S(2)}) %collective-permute-start.10) | collective-permute-done | bytes 67616 | tf_op jit(solution)/shard_map/ppermute | solution.py:33
  24.2 0.7 %collective-permute-start.9 = (bf16[1,264,128]{2,1,0:T(8,128)(2,1)S(1)}, bf16[1,264,128]{2,1,0:T(8,128)(2,1)S(1)}, u32[]{:S(2)}, u32[]{:S(2)}) collective-permute-start(bf16[1,264,128]{2,1,0:T(8,128)(2,1)S(1)} %get-tuple-element.28), channel_id=1, source_target_pairs={{0,1},{1,0},{2,3},{3,2},{4,5},{5,4},{6,7},{7,6},{8,9},{9,8},{10,11... | collective-permute-start | bytes 202760 | tf_op jit(solution)/shard_map/ppermute | solution.py:33
  25.0 0.0 collective-permute-done.11.refs_1_
  25.0 0.0 collective-permute-done.12.refs_2_
  25.0 2.5 %collective-permute-start.13 = (bf16[1,264,128]{2,1,0:T(8,128)(2,1)S(1)}, bf16[1,264,128]{2,1,0:T(8,128)(2,1)S(1)}, u32[]{:S(2)}, u32[]{:S(2)}) collective-permute-start(bf16[1,264,128]{2,1,0:T(8,128)(2,1)S(1)} %shard_map.40), channel_id=1, source_target_pairs={{0,2},{1,3},{2,0},{3,1},{4,6},{5,7},{6,4},{7,5},{8,10},{9,11},{10,... | collective-permute-start | bytes 202760 | tf_op jit(solution)/shard_map/ppermute | solution.py:33
  27.5 1.0 %shard_map.41 = (f32[256,256]{1,0:T(8,128)S(1)}, f32[256,256]{1,0:T(8,128)S(1)}) custom-call(bf16[256,256]{1,0:T(8,128)(2,1)S(1)} %get-tuple-element.22.own_ref.own, bf16[768,768]{1,0:T(8,128)(2,1)S(1)} %get-tuple-element.33.frame, bf16[2,256,256]{2,1,0:T(8,128)(2,1)S(1)} %get-tuple-element.34.crossed), custom_call_target="tpu_custom_call" | custom-call | flops 335544320 | tf_op jit(solution)/shard_map/pallas_call | solution.py:284
  28.5 0.0 collective-permute-done.7.refs_0_
  28.6 0.0 collective-permute-done.8.refs_1_
  28.6 0.3 %collective-permute-done.9.refs_2_ = bf16[1,264,128]{2,1,0:T(8,128)(2,1)S(1)} collective-permute-done((bf16[1,264,128]{2,1,0:T(8,128)(2,1)S(1)}, bf16[1,264,128]{2,1,0:T(8,128)(2,1)S(1)}, u32[]{:S(2)}, u32[]{:S(2)}) %collective-permute-start.9) | collective-permute-done | bytes 67616 | tf_op jit(solution)/shard_map/ppermute | solution.py:33
  28.9 1.8 %collective-permute-done.13.refs_3_ = bf16[1,264,128]{2,1,0:T(8,128)(2,1)S(1)} collective-permute-done((bf16[1,264,128]{2,1,0:T(8,128)(2,1)S(1)}, bf16[1,264,128]{2,1,0:T(8,128)(2,1)S(1)}, u32[]{:S(2)}, u32[]{:S(2)}) %collective-permute-start.13) | collective-permute-done | bytes 67616 | tf_op jit(solution)/shard_map/ppermute | solution.py:33
  30.7 0.8 %shard_map.42 = f32[1,256,256]{2,1,0:T(8,128)} custom-call(bf16[1,264,128]{2,1,0:T(8,128)(2,1)S(1)} %collective-permute-done.7.refs_0_, bf16[1,264,128]{2,1,0:T(8,128)(2,1)S(1)} %collective-permute-done.8.refs_1_, bf16[1,264,128]{2,1,0:T(8,128)(2,1)S(1)} %collective-permute-done.9.refs_2_, bf16[1,264,128]{2,1,0:T(8,128)(2,1)S(1)} %collective-permute-done.13.refs_3_, ...), custom_call_target="tpu_custom_call" | custom-call | flops 1000 | tf_op jit(solution)/shard_map/pallas_call | solution.py:284
  (1 shorter events, 0.0 us)
Async XLA Ops:
  0.0 0.9 %copy-start = (bf16[1,256,256]{2,1,0:T(8,128)(2,1)S(1)}, bf16[1,256,256]{2,1,0:T(8,128)(2,1)}, u32[]{:S(2)}) copy-start(bf16[1,256,256]{2,1,0:T(8,128)(2,1)} %ham.1) | copy-start | bytes 393220
  1.0 8.3 %collective-permute-start.1 = (bf16[1,264,128]{2,1,0:T(8,128)(2,1)S(1)}, bf16[1,264,128]{2,1,0:T(8,128)(2,1)S(1)}, u32[]{:S(2)}, u32[]{:S(2)}) collective-permute-start(bf16[1,264,128]{2,1,0:T(8,128)(2,1)S(1)} %get-tuple-element.21), channel_id=1, source_target_pairs={{2,0},{3,1},{0,2},{1,3},{6,4},{7,5},{4,6},{5,7},{10,8},{11,9},{8,1... | collective-permute-start | bytes 202760 | tf_op jit(solution)/shard_map/ppermute | solution.py:29
  5.1 7.1 %collective-permute-start.4 = (bf16[1,264,128]{2,1,0:T(8,128)(2,1)S(1)}, bf16[1,264,128]{2,1,0:T(8,128)(2,1)S(1)}, u32[]{:S(2)}, u32[]{:S(2)}) collective-permute-start(bf16[1,264,128]{2,1,0:T(8,128)(2,1)S(1)} %get-tuple-element.21), channel_id=1, source_target_pairs={{5,0},{4,1},{7,2},{6,3},{9,4},{8,5},{11,6},{10,7},{13,8},{12,9},{1... | collective-permute-start | bytes 202760 | tf_op jit(solution)/shard_map/ppermute | solution.py:29
  7.7 7.0 %collective-permute-start.3 = (bf16[1,264,128]{2,1,0:T(8,128)(2,1)S(1)}, bf16[1,264,128]{2,1,0:T(8,128)(2,1)S(1)}, u32[]{:S(2)}, u32[]{:S(2)}) collective-permute-start(bf16[1,264,128]{2,1,0:T(8,128)(2,1)S(1)} %get-tuple-element.21), channel_id=1, source_target_pairs={{4,0},{5,1},{6,2},{7,3},{8,4},{9,5},{10,6},{11,7},{12,8},{13,9},{1... | collective-permute-start | bytes 202760 | tf_op jit(solution)/shard_map/ppermute | solution.py:29
  8.8 5.8 %collective-permute-start = (bf16[1,264,128]{2,1,0:T(8,128)(2,1)S(1)}, bf16[1,264,128]{2,1,0:T(8,128)(2,1)S(1)}, u32[]{:S(2)}, u32[]{:S(2)}) collective-permute-start(bf16[1,264,128]{2,1,0:T(8,128)(2,1)S(1)} %get-tuple-element.21), channel_id=1, source_target_pairs={{1,0},{0,1},{3,2},{2,3},{5,4},{4,5},{7,6},{6,7},{9,8},{8,9},{11,10... | collective-permute-start | bytes 202760 | tf_op jit(solution)/shard_map/ppermute | solution.py:29
  9.3 5.4 %collective-permute-start.6 = (bf16[1,264,128]{2,1,0:T(8,128)(2,1)S(1)}, bf16[1,264,128]{2,1,0:T(8,128)(2,1)S(1)}, u32[]{:S(2)}, u32[]{:S(2)}) collective-permute-start(bf16[1,264,128]{2,1,0:T(8,128)(2,1)S(1)} %collective-permute-done.1.refs_1_), channel_id=1, source_target_pairs={{5,0},{4,1},{7,2},{6,3},{9,4},{8,5},{11,6},{10,7},{13,8},{12,9},{1... | collective-permute-start | bytes 202760 | tf_op jit(solution)/shard_map/ppermute | solution.py:29
  10.5 4.3 %collective-permute-start.5 = (bf16[1,264,128]{2,1,0:T(8,128)(2,1)S(1)}, bf16[1,264,128]{2,1,0:T(8,128)(2,1)S(1)}, u32[]{:S(2)}, u32[]{:S(2)}) collective-permute-start(bf16[1,264,128]{2,1,0:T(8,128)(2,1)S(1)} %collective-permute-done.1.refs_1_), channel_id=1, source_target_pairs={{4,0},{5,1},{6,2},{7,3},{8,4},{9,5},{10,6},{11,7},{12,8},{13,9},{1... | collective-permute-start | bytes 202760 | tf_op jit(solution)/shard_map/ppermute | solution.py:29
  12.2 4.3 %collective-permute-start.2 = (bf16[1,264,128]{2,1,0:T(8,128)(2,1)S(1)}, bf16[1,264,128]{2,1,0:T(8,128)(2,1)S(1)}, u32[]{:S(2)}, u32[]{:S(2)}) collective-permute-start(bf16[1,264,128]{2,1,0:T(8,128)(2,1)S(1)} %collective-permute-done.1.refs_1_), channel_id=1, source_target_pairs={{1,0},{0,1},{3,2},{2,3},{5,4},{4,5},{7,6},{6,7},{9,8},{8,9},{11,10... | collective-permute-start | bytes 202760 | tf_op jit(solution)/shard_map/ppermute | solution.py:29
  18.7 5.6 %collective-permute-start.10 = (bf16[1,264,128]{2,1,0:T(8,128)(2,1)S(1)}, bf16[1,264,128]{2,1,0:T(8,128)(2,1)S(1)}, u32[]{:S(2)}, u32[]{:S(2)}) collective-permute-start(bf16[1,264,128]{2,1,0:T(8,128)(2,1)S(1)} %get-tuple-element.29), channel_id=1, source_target_pairs={{0,5},{1,4},{2,7},{3,6},{4,9},{5,8},{6,11},{7,10},{8,13},{9,12},{1... | collective-permute-start | bytes 202760 | tf_op jit(solution)/shard_map/ppermute | solution.py:33
  18.7 6.2 %collective-permute-start.11 = (bf16[1,264,128]{2,1,0:T(8,128)(2,1)S(1)}, bf16[1,264,128]{2,1,0:T(8,128)(2,1)S(1)}, u32[]{:S(2)}, u32[]{:S(2)}) collective-permute-start(bf16[1,264,128]{2,1,0:T(8,128)(2,1)S(1)} %get-tuple-element.30), channel_id=1, source_target_pairs={{0,4},{1,5},{2,6},{3,7},{4,8},{5,9},{6,10},{7,11},{8,12},{9,13},{1... | collective-permute-start | bytes 202760 | tf_op jit(solution)/shard_map/ppermute | solution.py:33
  19.8 5.2 %collective-permute-start.12 = (bf16[1,264,128]{2,1,0:T(8,128)(2,1)S(1)}, bf16[1,264,128]{2,1,0:T(8,128)(2,1)S(1)}, u32[]{:S(2)}, u32[]{:S(2)}) collective-permute-start(bf16[1,264,128]{2,1,0:T(8,128)(2,1)S(1)} %get-tuple-element.31), channel_id=1, source_target_pairs={{0,1},{1,0},{2,3},{3,2},{4,5},{5,4},{6,7},{7,6},{8,9},{9,8},{10,11... | collective-permute-start | bytes 202760 | tf_op jit(solution)/shard_map/ppermute | solution.py:33
  20.8 7.8 %collective-permute-start.7 = (bf16[1,264,128]{2,1,0:T(8,128)(2,1)S(1)}, bf16[1,264,128]{2,1,0:T(8,128)(2,1)S(1)}, u32[]{:S(2)}, u32[]{:S(2)}) collective-permute-start(bf16[1,264,128]{2,1,0:T(8,128)(2,1)S(1)} %get-tuple-element.26), channel_id=1, source_target_pairs={{0,4},{1,5},{2,6},{3,7},{4,8},{5,9},{6,10},{7,11},{8,12},{9,13},{1... | collective-permute-start | bytes 202760 | tf_op jit(solution)/shard_map/ppermute | solution.py:33
  20.8 7.8 %collective-permute-start.8 = (bf16[1,264,128]{2,1,0:T(8,128)(2,1)S(1)}, bf16[1,264,128]{2,1,0:T(8,128)(2,1)S(1)}, u32[]{:S(2)}, u32[]{:S(2)}) collective-permute-start(bf16[1,264,128]{2,1,0:T(8,128)(2,1)S(1)} %get-tuple-element.27), channel_id=1, source_target_pairs={{0,5},{1,4},{2,7},{3,6},{4,9},{5,8},{6,11},{7,10},{8,13},{9,12},{1... | collective-permute-start | bytes 202760 | tf_op jit(solution)/shard_map/ppermute | solution.py:33
  24.2 4.7 %collective-permute-start.9 = (bf16[1,264,128]{2,1,0:T(8,128)(2,1)S(1)}, bf16[1,264,128]{2,1,0:T(8,128)(2,1)S(1)}, u32[]{:S(2)}, u32[]{:S(2)}) collective-permute-start(bf16[1,264,128]{2,1,0:T(8,128)(2,1)S(1)} %get-tuple-element.28), channel_id=1, source_target_pairs={{0,1},{1,0},{2,3},{3,2},{4,5},{5,4},{6,7},{7,6},{8,9},{9,8},{10,11... | collective-permute-start | bytes 202760 | tf_op jit(solution)/shard_map/ppermute | solution.py:33
  25.0 5.6 %collective-permute-start.13 = (bf16[1,264,128]{2,1,0:T(8,128)(2,1)S(1)}, bf16[1,264,128]{2,1,0:T(8,128)(2,1)S(1)}, u32[]{:S(2)}, u32[]{:S(2)}) collective-permute-start(bf16[1,264,128]{2,1,0:T(8,128)(2,1)S(1)} %shard_map.40), channel_id=1, source_target_pairs={{0,2},{1,3},{2,0},{3,1},{4,6},{5,7},{6,4},{7,5},{8,10},{9,11},{10,... | collective-permute-start | bytes 202760 | tf_op jit(solution)/shard_map/ppermute | solution.py:33

commit v3 on v2

--- a/solution.py
+++ b/solution.py
@@ -39,7 +39,7 @@
 
 def gather_plan(workers):
     if workers == 4:
-        return [(0, 2, None), (0, 1, None), (1, 1, None), (1, 0, None), (0, 1, 2), (1, 0, 2), (1, 1, 2)]
+        return [(0, 2, None), (0, 1, None), (1, 0, None), (0, 3, None), (1, 1, None), (1, 1, 2), (1, 0, 2)]
     return [(distance, k, None) for distance, k in everyone(workers)]
 
 
@@ -182,10 +182,10 @@
         return slice(i * n, (i + 1) * n)
 
     def chosen(candidates, first_row):
-        total = jnp.zeros((n + PAD, half), F32)
+        total = jnp.zeros((n + PAD, half), BF16)
         for c, ref in enumerate(candidates):
-            total = jnp.where(rows[first_row + c : first_row + c + 1, :] > 0.5, ref[0].astype(F32), total)
-        return total
+            total = total + ref[0] * rows[first_row + c : first_row + c + 1, :].astype(BF16)
+        return total.astype(F32)
 
     members = []
     for packed in (chosen(own + following, 0), chosen(following, 2 * workers - 1)):
@@ -210,7 +210,7 @@
     for (i, j), value in square.items():
         low[part(i), part(j)] = value.astype(BF16)
         if i < j:
-            low[part(j), part(i)] = value.T.astype(BF16)
+            low[part(j), part(i)] = value.astype(BF16).T
     products = {}
 
     def multiply(table, down, across):
@@ -226,24 +226,24 @@
         value = 3.0 * square[i, j] - 2.0 * products[i, j]
         frame[part(i), part(j)] = value.astype(BF16)
         if i < j:
-            frame[part(j), part(i)] = value.T.astype(BF16)
+            frame[part(j), part(i)] = value.astype(BF16).T
     product = dot(frame[: 2 * n, :], frame[:, n:])
     square = {(i, j): product[part(i), part(j - 1)] for i in (0, 1) for j in (1, 2)}
     square[2, 2] = dot(frame[2 * n :, :], frame[:, 2 * n :])
     for (i, j), value in square.items():
         low[part(i), part(j)] = value.astype(BF16)
-    low[part(2), part(1)] = square[1, 2].T.astype(BF16)
-    crossed[0] = square[0, 1].T.astype(BF16)
-    crossed[1] = square[0, 2].T.astype(BF16)
+    low[part(2), part(1)] = square[1, 2].astype(BF16).T
+    crossed[0] = square[0, 1].astype(BF16).T
+    crossed[1] = square[0, 2].astype(BF16).T
     pieces = []
     for s in (1, 2):
         density = 3.0 * square[s, s] - 2.0 * dot(frame[part(s), :], low[:, part(s)])
-        pieces.append(pack(density - members[s - 1]))
+        pieces.append(pack(density - members[s - 1]).astype(BF16))
     for at, ref in enumerate(sent):
-        value = jnp.where(rows[at : at + 1, :] > 0.5, pieces[0], 0.0)
+        value = pieces[0] * rows[at : at + 1, :].astype(BF16)
         if at >= workers - 1:
-            value = jnp.where(rows[at + workers : at + workers + 1, :] > 0.5, pieces[1], value)
-        ref[0] = value.astype(BF16)
+            value = value + pieces[1] * rows[at + workers : at + workers + 1, :].astype(BF16)
+        ref[0] = value
 
 
 def own_kernel(own, frame, crossed, mine, delta):

time: 31.6 us -> 31.6 us (level)
  waiting for transfers between devices: 5.45 us -> 6.17 us
  starting transfers between devices: 19 us -> 18.3 us
    ppermute x7, waiting for transfers between devices: 3.7 us -> 4.65 us  [to_mate(): return lax.ppermute(block, ('grp', 'wrk'), list(pairs(distance, k)))]
    ppermute x7, starting transfers between devices: 11.8 us -> 11.2 us  [from_mate(): lax.ppermute(block, ('grp', 'wrk'), [(there, here) for here, there in pai...]
  transfers between devices with their start and end apart: 14 -> 14, of which waited for: 4 -> 6; matrix products, arithmetic and copies ran while one was open for 0% -> 0% of each run, Pallas kernels for 9% -> 9%
where the time goes in v3:
time: 31.6 us; the launch traced here: 31.5 us
  starting transfers between devices  18.3 us (58%)
  waiting for transfers between devices  6.17 us (20%)
  Pallas kernels  6.02 us (19%)
  local copies, waits for them, and re-layouts  0.9 us (3%)
    ppermute x7, starting transfers between devices, from_mate(): lax.ppermute(block, ('grp', 'wrk'), [(there, here) for here, there in pai...  11.2 us
    ppermute x7, starting transfers between devices, to_mate(): return lax.ppermute(block, ('grp', 'wrk'), list(pairs(distance, k)))  7.08 us
    pallas_call x6, Pallas kernels, call(): pl.pallas_call(kernel, in_specs=[pl.BlockSpec(memory_space=pltpu.HBM)] *...  6.02 us
    ppermute x7, waiting for transfers between devices, to_mate(): return lax.ppermute(block, ('grp', 'wrk'), list(pairs(distance, k)))  4.65 us
    ppermute x7, waiting for transfers between devices, from_mate(): lax.ppermute(block, ('grp', 'wrk'), [(there, here) for here, there in pai...  1.52 us
    unnamed x2, local copies, waits for them, and re-layouts  0.9 us
  transfers between devices with their start and end apart: 14, of which 6 were waited for; matrix products, arithmetic and copies ran while one was open for 0% of the time, Pallas kernels for 9%

profile of v3, /device:TPU:0, one launch (start us, length us, event | category | flops | bytes accessed | tf_op | source)
XLA Modules:
  0.0 31.5 jit_solution(16843039230464413114)
XLA Ops:
  0.0 0.0 copy-start
  0.0 0.9 %copy-done = bf16[1,256,256]{2,1,0:T(8,128)(2,1)S(1)} copy-done((bf16[1,256,256]{2,1,0:T(8,128)(2,1)S(1)}, bf16[1,256,256]{2,1,0:T(8,128)(2,1)}, u32[]{:S(2)}) %copy-start) | copy-done | bytes 131096
  0.9 0.1 shard_map.37
  1.0 4.1 %collective-permute-start.1 = (bf16[1,264,128]{2,1,0:T(8,128)(2,1)S(1)}, bf16[1,264,128]{2,1,0:T(8,128)(2,1)S(1)}, u32[]{:S(2)}, u32[]{:S(2)}) collective-permute-start(bf16[1,264,128]{2,1,0:T(8,128)(2,1)S(1)} %get-tuple-element.21), channel_id=1, source_target_pairs={{2,0},{3,1},{0,2},{1,3},{6,4},{7,5},{4,6},{5,7},{10,8},{11,9},{8,1... | collective-permute-start | bytes 202760 | tf_op jit(solution)/shard_map/ppermute | solution.py:29
  5.1 2.6 %collective-permute-start.4 = (bf16[1,264,128]{2,1,0:T(8,128)(2,1)S(1)}, bf16[1,264,128]{2,1,0:T(8,128)(2,1)S(1)}, u32[]{:S(2)}, u32[]{:S(2)}) collective-permute-start(bf16[1,264,128]{2,1,0:T(8,128)(2,1)S(1)} %get-tuple-element.21), channel_id=1, source_target_pairs={{5,0},{4,1},{7,2},{6,3},{9,4},{8,5},{11,6},{10,7},{13,8},{12,9},{1... | collective-permute-start | bytes 202760 | tf_op jit(solution)/shard_map/ppermute | solution.py:29
  7.7 1.1 %collective-permute-start.3 = (bf16[1,264,128]{2,1,0:T(8,128)(2,1)S(1)}, bf16[1,264,128]{2,1,0:T(8,128)(2,1)S(1)}, u32[]{:S(2)}, u32[]{:S(2)}) collective-permute-start(bf16[1,264,128]{2,1,0:T(8,128)(2,1)S(1)} %get-tuple-element.21), channel_id=1, source_target_pairs={{4,0},{5,1},{6,2},{7,3},{8,4},{9,5},{10,6},{11,7},{12,8},{13,9},{1... | collective-permute-start | bytes 202760 | tf_op jit(solution)/shard_map/ppermute | solution.py:29
  8.8 0.2 collective-permute-start.2
  9.1 0.7 %collective-permute-start = (bf16[1,264,128]{2,1,0:T(8,128)(2,1)S(1)}, bf16[1,264,128]{2,1,0:T(8,128)(2,1)S(1)}, u32[]{:S(2)}, u32[]{:S(2)}) collective-permute-start(bf16[1,264,128]{2,1,0:T(8,128)(2,1)S(1)} %get-tuple-element.21), channel_id=1, source_target_pairs={{1,0},{0,1},{3,2},{2,3},{5,4},{4,5},{7,6},{6,7},{9,8},{8,9},{11,10... | collective-permute-start | bytes 202760 | tf_op jit(solution)/shard_map/ppermute | solution.py:29
  9.7 0.0 collective-permute-done.1.refs_1_
  9.7 0.7 %collective-permute-start.6 = (bf16[1,264,128]{2,1,0:T(8,128)(2,1)S(1)}, bf16[1,264,128]{2,1,0:T(8,128)(2,1)S(1)}, u32[]{:S(2)}, u32[]{:S(2)}) collective-permute-start(bf16[1,264,128]{2,1,0:T(8,128)(2,1)S(1)} %collective-permute-done.1.refs_1_), channel_id=1, source_target_pairs={{5,0},{4,1},{7,2},{6,3},{9,4},{8,5},{11,6},{10,7},{13,8},{12,9},{1... | collective-permute-start | bytes 202760 | tf_op jit(solution)/shard_map/ppermute | solution.py:29
  10.5 0.0 collective-permute-done.4.refs_4_
  10.5 1.8 %collective-permute-start.5 = (bf16[1,264,128]{2,1,0:T(8,128)(2,1)S(1)}, bf16[1,264,128]{2,1,0:T(8,128)(2,1)S(1)}, u32[]{:S(2)}, u32[]{:S(2)}) collective-permute-start(bf16[1,264,128]{2,1,0:T(8,128)(2,1)S(1)} %collective-permute-done.1.refs_1_), channel_id=1, source_target_pairs={{4,0},{5,1},{6,2},{7,3},{8,4},{9,5},{10,6},{11,7},{12,8},{13,9},{1... | collective-permute-start | bytes 202760 | tf_op jit(solution)/shard_map/ppermute | solution.py:29
  12.2 1.9 %shard_map.38 = (bf16[768,768]{1,0:T(8,128)(2,1)S(1)}, f32[768,768]{1,0:T(8,128)S(1)}, f32[11,128]{1,0:T(8,128)S(1)}) custom-call(s32[1,3]{1,0:T(1,128)} %members_hbm.1, bf16[1,3,256,256]{3,2,1,0:T(8,128)(2,1)} %coupling_hbm.1, bf16[256,256]{1,0:T(8,128)(2,1)S(1)} %get-tuple-element.22.own_ref.own), custom_call_target="tpu_custom_call" | custom-call | flops 603979776 | tf_op jit(solution)/shard_map/pallas_call | solution.py:284
  14.1 0.0 collective-permute-done.3.refs_3_
  14.1 0.9 %collective-permute-done.2.refs_2_ = bf16[1,264,128]{2,1,0:T(8,128)(2,1)S(1)} collective-permute-done((bf16[1,264,128]{2,1,0:T(8,128)(2,1)S(1)}, bf16[1,264,128]{2,1,0:T(8,128)(2,1)S(1)}, u32[]{:S(2)}, u32[]{:S(2)}) %collective-permute-start.2) | collective-permute-done | bytes 67616 | tf_op jit(solution)/shard_map/ppermute | solution.py:29
  15.0 0.4 %collective-permute-done.refs_0_ = bf16[1,264,128]{2,1,0:T(8,128)(2,1)S(1)} collective-permute-done((bf16[1,264,128]{2,1,0:T(8,128)(2,1)S(1)}, bf16[1,264,128]{2,1,0:T(8,128)(2,1)S(1)}, u32[]{:S(2)}, u32[]{:S(2)}) %collective-permute-start) | collective-permute-done | bytes 67616 | tf_op jit(solution)/shard_map/ppermute | solution.py:29
  15.4 0.2 collective-permute-done.6.refs_6_
  15.6 0.0 collective-permute-done.5.refs_5_
  15.6 2.2 %shard_map.39 = (bf16[1,264,128]{2,1,0:T(8,128)(2,1)S(1)}, bf16[1,264,128]{2,1,0:T(8,128)(2,1)S(1)}, bf16[1,264,128]{2,1,0:T(8,128)(2,1)S(1)}, bf16[1,264,128]{2...) custom-call(bf16[1,264,128]{2,1,0:T(8,128)(2,1)S(1)} %collective-per, ...), custom_call_target="tpu_custom_call" | custom-call | flops 1509949440 | tf_op jit(solution)/shard_map/pallas_call | solution.py:284
  17.8 0.1 collective-permute-start.10
  17.9 0.6 %collective-permute-start.11 = (bf16[1,264,128]{2,1,0:T(8,128)(2,1)S(1)}, bf16[1,264,128]{2,1,0:T(8,128)(2,1)S(1)}, u32[]{:S(2)}, u32[]{:S(2)}) collective-permute-start(bf16[1,264,128]{2,1,0:T(8,128)(2,1)S(1)} %get-tuple-element.30), channel_id=1, source_target_pairs={{0,4},{1,5},{2,6},{3,7},{4,8},{5,9},{6,10},{7,11},{8,12},{9,13},{1... | collective-permute-start | bytes 202760 | tf_op jit(solution)/shard_map/ppermute | solution.py:33
  18.5 1.0 %collective-permute-start.12 = (bf16[1,264,128]{2,1,0:T(8,128)(2,1)S(1)}, bf16[1,264,128]{2,1,0:T(8,128)(2,1)S(1)}, u32[]{:S(2)}, u32[]{:S(2)}) collective-permute-start(bf16[1,264,128]{2,1,0:T(8,128)(2,1)S(1)} %get-tuple-element.31), channel_id=1, source_target_pairs={{0,1},{1,0},{2,3},{3,2},{4,5},{5,4},{6,7},{7,6},{8,9},{9,8},{10,11... | collective-permute-start | bytes 202760 | tf_op jit(solution)/shard_map/ppermute | solution.py:33
  19.5 1.7 %collective-permute-start.7 = (bf16[1,264,128]{2,1,0:T(8,128)(2,1)S(1)}, bf16[1,264,128]{2,1,0:T(8,128)(2,1)S(1)}, u32[]{:S(2)}, u32[]{:S(2)}) collective-permute-start(bf16[1,264,128]{2,1,0:T(8,128)(2,1)S(1)} %get-tuple-element.26), channel_id=1, source_target_pairs={{0,4},{1,5},{2,6},{3,7},{4,8},{5,9},{6,10},{7,11},{8,12},{9,13},{1... | collective-permute-start | bytes 202760 | tf_op jit(solution)/shard_map/ppermute | solution.py:33
  21.2 1.0 %collective-permute-start.8 = (bf16[1,264,128]{2,1,0:T(8,128)(2,1)S(1)}, bf16[1,264,128]{2,1,0:T(8,128)(2,1)S(1)}, u32[]{:S(2)}, u32[]{:S(2)}) collective-permute-start(bf16[1,264,128]{2,1,0:T(8,128)(2,1)S(1)} %get-tuple-element.27), channel_id=1, source_target_pairs={{0,5},{1,4},{2,7},{3,6},{4,9},{5,8},{6,11},{7,10},{8,13},{9,12},{1... | collective-permute-start | bytes 202760 | tf_op jit(solution)/shard_map/ppermute | solution.py:33
  22.2 1.3 %collective-permute-done.10.refs_0_ = bf16[1,264,128]{2,1,0:T(8,128)(2,1)S(1)} collective-permute-done((bf16[1,264,128]{2,1,0:T(8,128)(2,1)S(1)}, bf16[1,264,128]{2,1,0:T(8,128)(2,1)S(1)}, u32[]{:S(2)}, u32[]{:S(2)}) %collective-permute-start.10) | collective-permute-done | bytes 67616 | tf_op jit(solution)/shard_map/ppermute | solution.py:33
  23.5 0.8 %collective-permute-start.9 = (bf16[1,264,128]{2,1,0:T(8,128)(2,1)S(1)}, bf16[1,264,128]{2,1,0:T(8,128)(2,1)S(1)}, u32[]{:S(2)}, u32[]{:S(2)}) collective-permute-start(bf16[1,264,128]{2,1,0:T(8,128)(2,1)S(1)} %get-tuple-element.28), channel_id=1, source_target_pairs={{0,1},{1,0},{2,3},{3,2},{4,5},{5,4},{6,7},{7,6},{8,9},{9,8},{10,11... | collective-permute-start | bytes 202760 | tf_op jit(solution)/shard_map/ppermute | solution.py:33
  24.3 0.0 collective-permute-done.11.refs_1_
  24.3 0.0 collective-permute-done.12.refs_2_
  24.4 1.9 %collective-permute-start.13 = (bf16[1,264,128]{2,1,0:T(8,128)(2,1)S(1)}, bf16[1,264,128]{2,1,0:T(8,128)(2,1)S(1)}, u32[]{:S(2)}, u32[]{:S(2)}) collective-permute-start(bf16[1,264,128]{2,1,0:T(8,128)(2,1)S(1)} %shard_map.40), channel_id=1, source_target_pairs={{0,2},{1,3},{2,0},{3,1},{4,6},{5,7},{6,4},{7,5},{8,10},{9,11},{10,... | collective-permute-start | bytes 202760 | tf_op jit(solution)/shard_map/ppermute | solution.py:33
  26.3 1.0 %shard_map.41 = (f32[256,256]{1,0:T(8,128)S(1)}, f32[256,256]{1,0:T(8,128)S(1)}) custom-call(bf16[256,256]{1,0:T(8,128)(2,1)S(1)} %get-tuple-element.22.own_ref.own, bf16[768,768]{1,0:T(8,128)(2,1)S(1)} %get-tuple-element.33.frame, bf16[2,256,256]{2,1,0:T(8,128)(2,1)S(1)} %get-tuple-element.34.crossed), custom_call_target="tpu_custom_call" | custom-call | flops 335544320 | tf_op jit(solution)/shard_map/pallas_call | solution.py:284
  27.3 0.0 collective-permute-done.7.refs_0_
  27.3 0.0 collective-permute-done.8.refs_1_
  27.3 1.2 %collective-permute-done.9.refs_2_ = bf16[1,264,128]{2,1,0:T(8,128)(2,1)S(1)} collective-permute-done((bf16[1,264,128]{2,1,0:T(8,128)(2,1)S(1)}, bf16[1,264,128]{2,1,0:T(8,128)(2,1)S(1)}, u32[]{:S(2)}, u32[]{:S(2)}) %collective-permute-start.9) | collective-permute-done | bytes 67616 | tf_op jit(solution)/shard_map/ppermute | solution.py:33
  28.5 2.2 %collective-permute-done.13.refs_3_ = bf16[1,264,128]{2,1,0:T(8,128)(2,1)S(1)} collective-permute-done((bf16[1,264,128]{2,1,0:T(8,128)(2,1)S(1)}, bf16[1,264,128]{2,1,0:T(8,128)(2,1)S(1)}, u32[]{:S(2)}, u32[]{:S(2)}) %collective-permute-start.13) | collective-permute-done | bytes 67616 | tf_op jit(solution)/shard_map/ppermute | solution.py:33
  30.7 0.8 %shard_map.42 = f32[1,256,256]{2,1,0:T(8,128)} custom-call(bf16[1,264,128]{2,1,0:T(8,128)(2,1)S(1)} %collective-permute-done.7.refs_0_, bf16[1,264,128]{2,1,0:T(8,128)(2,1)S(1)} %collective-permute-done.8.refs_1_, bf16[1,264,128]{2,1,0:T(8,128)(2,1)S(1)} %collective-permute-done.9.refs_2_, bf16[1,264,128]{2,1,0:T(8,128)(2,1)S(1)} %collective-permute-done.13.refs_3_, ...), custom_call_target="tpu_custom_call" | custom-call | flops 1000 | tf_op jit(solution)/shard_map/pallas_call | solution.py:284
  (1 shorter events, 0.0 us)
Async XLA Ops:
  0.0 0.9 %copy-start = (bf16[1,256,256]{2,1,0:T(8,128)(2,1)S(1)}, bf16[1,256,256]{2,1,0:T(8,128)(2,1)}, u32[]{:S(2)}) copy-start(bf16[1,256,256]{2,1,0:T(8,128)(2,1)} %ham.1) | copy-start | bytes 393220
  1.0 8.8 %collective-permute-start.1 = (bf16[1,264,128]{2,1,0:T(8,128)(2,1)S(1)}, bf16[1,264,128]{2,1,0:T(8,128)(2,1)S(1)}, u32[]{:S(2)}, u32[]{:S(2)}) collective-permute-start(bf16[1,264,128]{2,1,0:T(8,128)(2,1)S(1)} %get-tuple-element.21), channel_id=1, source_target_pairs={{2,0},{3,1},{0,2},{1,3},{6,4},{7,5},{4,6},{5,7},{10,8},{11,9},{8,1... | collective-permute-start | bytes 202760 | tf_op jit(solution)/shard_map/ppermute | solution.py:29
  5.1 5.4 %collective-permute-start.4 = (bf16[1,264,128]{2,1,0:T(8,128)(2,1)S(1)}, bf16[1,264,128]{2,1,0:T(8,128)(2,1)S(1)}, u32[]{:S(2)}, u32[]{:S(2)}) collective-permute-start(bf16[1,264,128]{2,1,0:T(8,128)(2,1)S(1)} %get-tuple-element.21), channel_id=1, source_target_pairs={{5,0},{4,1},{7,2},{6,3},{9,4},{8,5},{11,6},{10,7},{13,8},{12,9},{1... | collective-permute-start | bytes 202760 | tf_op jit(solution)/shard_map/ppermute | solution.py:29
  7.7 6.4 %collective-permute-start.3 = (bf16[1,264,128]{2,1,0:T(8,128)(2,1)S(1)}, bf16[1,264,128]{2,1,0:T(8,128)(2,1)S(1)}, u32[]{:S(2)}, u32[]{:S(2)}) collective-permute-start(bf16[1,264,128]{2,1,0:T(8,128)(2,1)S(1)} %get-tuple-element.21), channel_id=1, source_target_pairs={{4,0},{5,1},{6,2},{7,3},{8,4},{9,5},{10,6},{11,7},{12,8},{13,9},{1... | collective-permute-start | bytes 202760 | tf_op jit(solution)/shard_map/ppermute | solution.py:29
  8.8 6.2 %collective-permute-start.2 = (bf16[1,264,128]{2,1,0:T(8,128)(2,1)S(1)}, bf16[1,264,128]{2,1,0:T(8,128)(2,1)S(1)}, u32[]{:S(2)}, u32[]{:S(2)}) collective-permute-start(bf16[1,264,128]{2,1,0:T(8,128)(2,1)S(1)} %get-tuple-element.21), channel_id=1, source_target_pairs={{3,0},{2,1},{1,2},{0,3},{7,4},{6,5},{5,6},{4,7},{11,8},{10,9},{9,1... | collective-permute-start | bytes 202760 | tf_op jit(solution)/shard_map/ppermute | solution.py:29
  9.1 6.4 %collective-permute-start = (bf16[1,264,128]{2,1,0:T(8,128)(2,1)S(1)}, bf16[1,264,128]{2,1,0:T(8,128)(2,1)S(1)}, u32[]{:S(2)}, u32[]{:S(2)}) collective-permute-start(bf16[1,264,128]{2,1,0:T(8,128)(2,1)S(1)} %get-tuple-element.21), channel_id=1, source_target_pairs={{1,0},{0,1},{3,2},{2,3},{5,4},{4,5},{7,6},{6,7},{9,8},{8,9},{11,10... | collective-permute-start | bytes 202760 | tf_op jit(solution)/shard_map/ppermute | solution.py:29
  9.7 5.9 %collective-permute-start.6 = (bf16[1,264,128]{2,1,0:T(8,128)(2,1)S(1)}, bf16[1,264,128]{2,1,0:T(8,128)(2,1)S(1)}, u32[]{:S(2)}, u32[]{:S(2)}) collective-permute-start(bf16[1,264,128]{2,1,0:T(8,128)(2,1)S(1)} %collective-permute-done.1.refs_1_), channel_id=1, source_target_pairs={{5,0},{4,1},{7,2},{6,3},{9,4},{8,5},{11,6},{10,7},{13,8},{12,9},{1... | collective-permute-start | bytes 202760 | tf_op jit(solution)/shard_map/ppermute | solution.py:29
  10.5 5.2 %collective-permute-start.5 = (bf16[1,264,128]{2,1,0:T(8,128)(2,1)S(1)}, bf16[1,264,128]{2,1,0:T(8,128)(2,1)S(1)}, u32[]{:S(2)}, u32[]{:S(2)}) collective-permute-start(bf16[1,264,128]{2,1,0:T(8,128)(2,1)S(1)} %collective-permute-done.1.refs_1_), channel_id=1, source_target_pairs={{4,0},{5,1},{6,2},{7,3},{8,4},{9,5},{10,6},{11,7},{12,8},{13,9},{1... | collective-permute-start | bytes 202760 | tf_op jit(solution)/shard_map/ppermute | solution.py:29
  17.8 5.7 %collective-permute-start.10 = (bf16[1,264,128]{2,1,0:T(8,128)(2,1)S(1)}, bf16[1,264,128]{2,1,0:T(8,128)(2,1)S(1)}, u32[]{:S(2)}, u32[]{:S(2)}) collective-permute-start(bf16[1,264,128]{2,1,0:T(8,128)(2,1)S(1)} %get-tuple-element.29), channel_id=1, source_target_pairs={{0,5},{1,4},{2,7},{3,6},{4,9},{5,8},{6,11},{7,10},{8,13},{9,12},{1... | collective-permute-start | bytes 202760 | tf_op jit(solution)/shard_map/ppermute | solution.py:33
  17.9 6.4 %collective-permute-start.11 = (bf16[1,264,128]{2,1,0:T(8,128)(2,1)S(1)}, bf16[1,264,128]{2,1,0:T(8,128)(2,1)S(1)}, u32[]{:S(2)}, u32[]{:S(2)}) collective-permute-start(bf16[1,264,128]{2,1,0:T(8,128)(2,1)S(1)} %get-tuple-element.30), channel_id=1, source_target_pairs={{0,4},{1,5},{2,6},{3,7},{4,8},{5,9},{6,10},{7,11},{8,12},{9,13},{1... | collective-permute-start | bytes 202760 | tf_op jit(solution)/shard_map/ppermute | solution.py:33
  18.5 5.8 %collective-permute-start.12 = (bf16[1,264,128]{2,1,0:T(8,128)(2,1)S(1)}, bf16[1,264,128]{2,1,0:T(8,128)(2,1)S(1)}, u32[]{:S(2)}, u32[]{:S(2)}) collective-permute-start(bf16[1,264,128]{2,1,0:T(8,128)(2,1)S(1)} %get-tuple-element.31), channel_id=1, source_target_pairs={{0,1},{1,0},{2,3},{3,2},{4,5},{5,4},{6,7},{7,6},{8,9},{9,8},{10,11... | collective-permute-start | bytes 202760 | tf_op jit(solution)/shard_map/ppermute | solution.py:33
  19.5 7.9 %collective-permute-start.7 = (bf16[1,264,128]{2,1,0:T(8,128)(2,1)S(1)}, bf16[1,264,128]{2,1,0:T(8,128)(2,1)S(1)}, u32[]{:S(2)}, u32[]{:S(2)}) collective-permute-start(bf16[1,264,128]{2,1,0:T(8,128)(2,1)S(1)} %get-tuple-element.26), channel_id=1, source_target_pairs={{0,4},{1,5},{2,6},{3,7},{4,8},{5,9},{6,10},{7,11},{8,12},{9,13},{1... | collective-permute-start | bytes 202760 | tf_op jit(solution)/shard_map/ppermute | solution.py:33
  21.2 6.1 %collective-permute-start.8 = (bf16[1,264,128]{2,1,0:T(8,128)(2,1)S(1)}, bf16[1,264,128]{2,1,0:T(8,128)(2,1)S(1)}, u32[]{:S(2)}, u32[]{:S(2)}) collective-permute-start(bf16[1,264,128]{2,1,0:T(8,128)(2,1)S(1)} %get-tuple-element.27), channel_id=1, source_target_pairs={{0,5},{1,4},{2,7},{3,6},{4,9},{5,8},{6,11},{7,10},{8,13},{9,12},{1... | collective-permute-start | bytes 202760 | tf_op jit(solution)/shard_map/ppermute | solution.py:33
  23.5 5.0 %collective-permute-start.9 = (bf16[1,264,128]{2,1,0:T(8,128)(2,1)S(1)}, bf16[1,264,128]{2,1,0:T(8,128)(2,1)S(1)}, u32[]{:S(2)}, u32[]{:S(2)}) collective-permute-start(bf16[1,264,128]{2,1,0:T(8,128)(2,1)S(1)} %get-tuple-element.28), channel_id=1, source_target_pairs={{0,1},{1,0},{2,3},{3,2},{4,5},{5,4},{6,7},{7,6},{8,9},{9,8},{10,11... | collective-permute-start | bytes 202760 | tf_op jit(solution)/shard_map/ppermute | solution.py:33
  24.4 6.3 %collective-permute-start.13 = (bf16[1,264,128]{2,1,0:T(8,128)(2,1)S(1)}, bf16[1,264,128]{2,1,0:T(8,128)(2,1)S(1)}, u32[]{:S(2)}, u32[]{:S(2)}) collective-permute-start(bf16[1,264,128]{2,1,0:T(8,128)(2,1)S(1)} %shard_map.40), channel_id=1, source_target_pairs={{0,2},{1,3},{2,0},{3,1},{4,6},{5,7},{6,4},{7,5},{8,10},{9,11},{10,... | collective-permute-start | bytes 202760 | tf_op jit(solution)/shard_map/ppermute | solution.py:33

commit v4 on v2

--- a/solution.py
+++ b/solution.py
@@ -164,9 +164,10 @@
     frame[2 * n :, :n] = c02.T.astype(BF16)
     frame[2 * n :, n : 2 * n] = c12.T.astype(BF16)
     frame[2 * n :, 2 * n :] = jnp.zeros((n, n), BF16)
-    for j in range(3):
-        part = slice(j * n, (j + 1) * n)
-        known[: (j + 1) * n, part] = dot(frame[: (j + 1) * n, :], frame[:, part])
+    known[:n, :n] = dot(frame[:n, :], frame[:, :n])
+    known[:, 2 * n :] = dot(frame[:, : 2 * n], frame[: 2 * n, 2 * n :])
+    left = dot(frame[: 2 * n, :n], frame[:n, n : 2 * n])
+    known[: 2 * n, n : 2 * n] = left + dot(frame[: 2 * n, 2 * n :], frame[2 * n :, n : 2 * n])
 
 
 def main_kernel(*refs, workers):

time: 31.6 us -> 31.6 us (level)
  no operation moved by 1% of the time
where the time goes in v4:
time: 31.6 us; the launch traced here: 31.5 us
  starting transfers between devices  19 us (60%)
  Pallas kernels  5.92 us (19%)
  waiting for transfers between devices  5.57 us (18%)
  local copies, waits for them, and re-layouts  0.9 us (3%)
    ppermute x7, starting transfers between devices, from_mate(): lax.ppermute(block, ('grp', 'wrk'), [(there, here) for here, there in pai...  11.8 us
    ppermute x7, starting transfers between devices, to_mate(): return lax.ppermute(block, ('grp', 'wrk'), list(pairs(distance, k)))  7.15 us
    pallas_call x6, Pallas kernels, call(): pl.pallas_call(kernel, in_specs=[pl.BlockSpec(memory_space=pltpu.HBM)] *...  5.92 us
    ppermute x7, waiting for transfers between devices, to_mate(): return lax.ppermute(block, ('grp', 'wrk'), list(pairs(distance, k)))  3.7 us
    ppermute x7, waiting for transfers between devices, from_mate(): lax.ppermute(block, ('grp', 'wrk'), [(there, here) for here, there in pai...  1.86 us
    unnamed x2, local copies, waits for them, and re-layouts  0.9 us
  transfers between devices with their start and end apart: 14, of which 4 were waited for; matrix products, arithmetic and copies ran while one was open for 0% of the time, Pallas kernels for 9%

profile of v4, /device:TPU:0, one launch (start us, length us, event | category | flops | bytes accessed | tf_op | source)
XLA Modules:
  0.0 31.5 jit_solution(17669854454501934378)
XLA Ops:
  0.0 0.0 copy-start
  0.0 0.9 %copy-done = bf16[1,256,256]{2,1,0:T(8,128)(2,1)S(1)} copy-done((bf16[1,256,256]{2,1,0:T(8,128)(2,1)S(1)}, bf16[1,256,256]{2,1,0:T(8,128)(2,1)}, u32[]{:S(2)}) %copy-start) | copy-done | bytes 131096
  0.9 0.1 shard_map.37
  1.0 4.1 %collective-permute-start.1 = (bf16[1,264,128]{2,1,0:T(8,128)(2,1)S(1)}, bf16[1,264,128]{2,1,0:T(8,128)(2,1)S(1)}, u32[]{:S(2)}, u32[]{:S(2)}) collective-permute-start(bf16[1,264,128]{2,1,0:T(8,128)(2,1)S(1)} %get-tuple-element.21), channel_id=1, source_target_pairs={{2,0},{3,1},{0,2},{1,3},{6,4},{7,5},{4,6},{5,7},{10,8},{11,9},{8,1... | collective-permute-start | bytes 202760 | tf_op jit(solution)/shard_map/ppermute | solution.py:29
  5.1 2.6 %collective-permute-start.4 = (bf16[1,264,128]{2,1,0:T(8,128)(2,1)S(1)}, bf16[1,264,128]{2,1,0:T(8,128)(2,1)S(1)}, u32[]{:S(2)}, u32[]{:S(2)}) collective-permute-start(bf16[1,264,128]{2,1,0:T(8,128)(2,1)S(1)} %get-tuple-element.21), channel_id=1, source_target_pairs={{5,0},{4,1},{7,2},{6,3},{9,4},{8,5},{11,6},{10,7},{13,8},{12,9},{1... | collective-permute-start | bytes 202760 | tf_op jit(solution)/shard_map/ppermute | solution.py:29
  7.7 1.1 %collective-permute-start.3 = (bf16[1,264,128]{2,1,0:T(8,128)(2,1)S(1)}, bf16[1,264,128]{2,1,0:T(8,128)(2,1)S(1)}, u32[]{:S(2)}, u32[]{:S(2)}) collective-permute-start(bf16[1,264,128]{2,1,0:T(8,128)(2,1)S(1)} %get-tuple-element.21), channel_id=1, source_target_pairs={{4,0},{5,1},{6,2},{7,3},{8,4},{9,5},{10,6},{11,7},{12,8},{13,9},{1... | collective-permute-start | bytes 202760 | tf_op jit(solution)/shard_map/ppermute | solution.py:29
  8.8 0.4 %collective-permute-start = (bf16[1,264,128]{2,1,0:T(8,128)(2,1)S(1)}, bf16[1,264,128]{2,1,0:T(8,128)(2,1)S(1)}, u32[]{:S(2)}, u32[]{:S(2)}) collective-permute-start(bf16[1,264,128]{2,1,0:T(8,128)(2,1)S(1)} %get-tuple-element.21), channel_id=1, source_target_pairs={{1,0},{0,1},{3,2},{2,3},{5,4},{4,5},{7,6},{6,7},{9,8},{8,9},{11,10... | collective-permute-start | bytes 202760 | tf_op jit(solution)/shard_map/ppermute | solution.py:29
  9.3 0.0 collective-permute-done.1.refs_1_
  9.3 1.2 %collective-permute-start.6 = (bf16[1,264,128]{2,1,0:T(8,128)(2,1)S(1)}, bf16[1,264,128]{2,1,0:T(8,128)(2,1)S(1)}, u32[]{:S(2)}, u32[]{:S(2)}) collective-permute-start(bf16[1,264,128]{2,1,0:T(8,128)(2,1)S(1)} %collective-permute-done.1.refs_1_), channel_id=1, source_target_pairs={{5,0},{4,1},{7,2},{6,3},{9,4},{8,5},{11,6},{10,7},{13,8},{12,9},{1... | collective-permute-start | bytes 202760 | tf_op jit(solution)/shard_map/ppermute | solution.py:29
  10.5 1.7 %collective-permute-start.5 = (bf16[1,264,128]{2,1,0:T(8,128)(2,1)S(1)}, bf16[1,264,128]{2,1,0:T(8,128)(2,1)S(1)}, u32[]{:S(2)}, u32[]{:S(2)}) collective-permute-start(bf16[1,264,128]{2,1,0:T(8,128)(2,1)S(1)} %collective-permute-done.1.refs_1_), channel_id=1, source_target_pairs={{4,0},{5,1},{6,2},{7,3},{8,4},{9,5},{10,6},{11,7},{12,8},{13,9},{1... | collective-permute-start | bytes 202760 | tf_op jit(solution)/shard_map/ppermute | solution.py:29
  12.2 0.0 collective-permute-done.4.refs_4_
  12.2 0.6 %collective-permute-start.2 = (bf16[1,264,128]{2,1,0:T(8,128)(2,1)S(1)}, bf16[1,264,128]{2,1,0:T(8,128)(2,1)S(1)}, u32[]{:S(2)}, u32[]{:S(2)}) collective-permute-start(bf16[1,264,128]{2,1,0:T(8,128)(2,1)S(1)} %collective-permute-done.1.refs_1_), channel_id=1, source_target_pairs={{1,0},{0,1},{3,2},{2,3},{5,4},{4,5},{7,6},{6,7},{9,8},{8,9},{11,10... | collective-permute-start | bytes 202760 | tf_op jit(solution)/shard_map/ppermute | solution.py:29
  12.8 1.8 %shard_map.38 = (bf16[768,768]{1,0:T(8,128)(2,1)S(1)}, f32[768,768]{1,0:T(8,128)S(1)}, f32[11,128]{1,0:T(8,128)S(1)}) custom-call(s32[1,3]{1,0:T(1,128)} %members_hbm.1, bf16[1,3,256,256]{3,2,1,0:T(8,128)(2,1)} %coupling_hbm.1, bf16[256,256]{1,0:T(8,128)(2,1)S(1)} %get-tuple-element.22.own_ref.own), custom_call_target="tpu_custom_call" | custom-call | flops 603979776 | tf_op jit(solution)/shard_map/pallas_call | solution.py:285
  14.6 0.0 collective-permute-done.3.refs_3_
  14.6 0.0 collective-permute-done.refs_0_
  14.6 0.0 collective-permute-done.6.refs_6_
  14.6 0.0 collective-permute-done.5.refs_5_
  14.6 1.8 %collective-permute-done.2.refs_2_ = bf16[1,264,128]{2,1,0:T(8,128)(2,1)S(1)} collective-permute-done((bf16[1,264,128]{2,1,0:T(8,128)(2,1)S(1)}, bf16[1,264,128]{2,1,0:T(8,128)(2,1)S(1)}, u32[]{:S(2)}, u32[]{:S(2)}) %collective-permute-start.2) | collective-permute-done | bytes 67616 | tf_op jit(solution)/shard_map/ppermute | solution.py:29
  16.5 2.2 %shard_map.39 = (bf16[1,264,128]{2,1,0:T(8,128)(2,1)S(1)}, bf16[1,264,128]{2,1,0:T(8,128)(2,1)S(1)}, bf16[1,264,128]{2,1,0:T(8,128)(2,1)S(1)}, bf16[1,264,128]{2...) custom-call(bf16[1,264,128]{2,1,0:T(8,128)(2,1)S(1)} %collective-per, ...), custom_call_target="tpu_custom_call" | custom-call | flops 1509949440 | tf_op jit(solution)/shard_map/pallas_call | solution.py:285
  18.7 0.1 collective-permute-start.10
  18.7 1.1 %collective-permute-start.11 = (bf16[1,264,128]{2,1,0:T(8,128)(2,1)S(1)}, bf16[1,264,128]{2,1,0:T(8,128)(2,1)S(1)}, u32[]{:S(2)}, u32[]{:S(2)}) collective-permute-start(bf16[1,264,128]{2,1,0:T(8,128)(2,1)S(1)} %get-tuple-element.30), channel_id=1, source_target_pairs={{0,4},{1,5},{2,6},{3,7},{4,8},{5,9},{6,10},{7,11},{8,12},{9,13},{1... | collective-permute-start | bytes 202760 | tf_op jit(solution)/shard_map/ppermute | solution.py:33
  19.8 0.9 %collective-permute-start.12 = (bf16[1,264,128]{2,1,0:T(8,128)(2,1)S(1)}, bf16[1,264,128]{2,1,0:T(8,128)(2,1)S(1)}, u32[]{:S(2)}, u32[]{:S(2)}) collective-permute-start(bf16[1,264,128]{2,1,0:T(8,128)(2,1)S(1)} %get-tuple-element.31), channel_id=1, source_target_pairs={{0,1},{1,0},{2,3},{3,2},{4,5},{5,4},{6,7},{7,6},{8,9},{9,8},{10,11... | collective-permute-start | bytes 202760 | tf_op jit(solution)/shard_map/ppermute | solution.py:33
  20.8 0.0 collective-permute-start.7
  20.8 1.9 %collective-permute-start.8 = (bf16[1,264,128]{2,1,0:T(8,128)(2,1)S(1)}, bf16[1,264,128]{2,1,0:T(8,128)(2,1)S(1)}, u32[]{:S(2)}, u32[]{:S(2)}) collective-permute-start(bf16[1,264,128]{2,1,0:T(8,128)(2,1)S(1)} %get-tuple-element.27), channel_id=1, source_target_pairs={{0,5},{1,4},{2,7},{3,6},{4,9},{5,8},{6,11},{7,10},{8,13},{9,12},{1... | collective-permute-start | bytes 202760 | tf_op jit(solution)/shard_map/ppermute | solution.py:33
  22.6 1.6 %collective-permute-done.10.refs_0_ = bf16[1,264,128]{2,1,0:T(8,128)(2,1)S(1)} collective-permute-done((bf16[1,264,128]{2,1,0:T(8,128)(2,1)S(1)}, bf16[1,264,128]{2,1,0:T(8,128)(2,1)S(1)}, u32[]{:S(2)}, u32[]{:S(2)}) %collective-permute-start.10) | collective-permute-done | bytes 67616 | tf_op jit(solution)/shard_map/ppermute | solution.py:33
  24.2 0.7 %collective-permute-start.9 = (bf16[1,264,128]{2,1,0:T(8,128)(2,1)S(1)}, bf16[1,264,128]{2,1,0:T(8,128)(2,1)S(1)}, u32[]{:S(2)}, u32[]{:S(2)}) collective-permute-start(bf16[1,264,128]{2,1,0:T(8,128)(2,1)S(1)} %get-tuple-element.28), channel_id=1, source_target_pairs={{0,1},{1,0},{2,3},{3,2},{4,5},{5,4},{6,7},{7,6},{8,9},{9,8},{10,11... | collective-permute-start | bytes 202760 | tf_op jit(solution)/shard_map/ppermute | solution.py:33
  25.0 0.0 collective-permute-done.11.refs_1_
  25.0 0.0 collective-permute-done.12.refs_2_
  25.0 2.5 %collective-permute-start.13 = (bf16[1,264,128]{2,1,0:T(8,128)(2,1)S(1)}, bf16[1,264,128]{2,1,0:T(8,128)(2,1)S(1)}, u32[]{:S(2)}, u32[]{:S(2)}) collective-permute-start(bf16[1,264,128]{2,1,0:T(8,128)(2,1)S(1)} %shard_map.40), channel_id=1, source_target_pairs={{0,2},{1,3},{2,0},{3,1},{4,6},{5,7},{6,4},{7,5},{8,10},{9,11},{10,... | collective-permute-start | bytes 202760 | tf_op jit(solution)/shard_map/ppermute | solution.py:33
  27.5 1.0 %shard_map.41 = (f32[256,256]{1,0:T(8,128)S(1)}, f32[256,256]{1,0:T(8,128)S(1)}) custom-call(bf16[256,256]{1,0:T(8,128)(2,1)S(1)} %get-tuple-element.22.own_ref.own, bf16[768,768]{1,0:T(8,128)(2,1)S(1)} %get-tuple-element.33.frame, bf16[2,256,256]{2,1,0:T(8,128)(2,1)S(1)} %get-tuple-element.34.crossed), custom_call_target="tpu_custom_call" | custom-call | flops 335544320 | tf_op jit(solution)/shard_map/pallas_call | solution.py:285
  28.5 0.0 collective-permute-done.7.refs_0_
  28.6 0.0 collective-permute-done.8.refs_1_
  28.6 0.3 %collective-permute-done.9.refs_2_ = bf16[1,264,128]{2,1,0:T(8,128)(2,1)S(1)} collective-permute-done((bf16[1,264,128]{2,1,0:T(8,128)(2,1)S(1)}, bf16[1,264,128]{2,1,0:T(8,128)(2,1)S(1)}, u32[]{:S(2)}, u32[]{:S(2)}) %collective-permute-start.9) | collective-permute-done | bytes 67616 | tf_op jit(solution)/shard_map/ppermute | solution.py:33
  28.9 1.8 %collective-permute-done.13.refs_3_ = bf16[1,264,128]{2,1,0:T(8,128)(2,1)S(1)} collective-permute-done((bf16[1,264,128]{2,1,0:T(8,128)(2,1)S(1)}, bf16[1,264,128]{2,1,0:T(8,128)(2,1)S(1)}, u32[]{:S(2)}, u32[]{:S(2)}) %collective-permute-start.13) | collective-permute-done | bytes 67616 | tf_op jit(solution)/shard_map/ppermute | solution.py:33
  30.7 0.8 %shard_map.42 = f32[1,256,256]{2,1,0:T(8,128)} custom-call(bf16[1,264,128]{2,1,0:T(8,128)(2,1)S(1)} %collective-permute-done.7.refs_0_, bf16[1,264,128]{2,1,0:T(8,128)(2,1)S(1)} %collective-permute-done.8.refs_1_, bf16[1,264,128]{2,1,0:T(8,128)(2,1)S(1)} %collective-permute-done.9.refs_2_, bf16[1,264,128]{2,1,0:T(8,128)(2,1)S(1)} %collective-permute-done.13.refs_3_, ...), custom_call_target="tpu_custom_call" | custom-call | flops 1000 | tf_op jit(solution)/shard_map/pallas_call | solution.py:285
  (1 shorter events, 0.0 us)
Async XLA Ops:
  0.0 0.9 %copy-start = (bf16[1,256,256]{2,1,0:T(8,128)(2,1)S(1)}, bf16[1,256,256]{2,1,0:T(8,128)(2,1)}, u32[]{:S(2)}) copy-start(bf16[1,256,256]{2,1,0:T(8,128)(2,1)} %ham.1) | copy-start | bytes 393220
  1.0 8.3 %collective-permute-start.1 = (bf16[1,264,128]{2,1,0:T(8,128)(2,1)S(1)}, bf16[1,264,128]{2,1,0:T(8,128)(2,1)S(1)}, u32[]{:S(2)}, u32[]{:S(2)}) collective-permute-start(bf16[1,264,128]{2,1,0:T(8,128)(2,1)S(1)} %get-tuple-element.21), channel_id=1, source_target_pairs={{2,0},{3,1},{0,2},{1,3},{6,4},{7,5},{4,6},{5,7},{10,8},{11,9},{8,1... | collective-permute-start | bytes 202760 | tf_op jit(solution)/shard_map/ppermute | solution.py:29
  5.1 7.1 %collective-permute-start.4 = (bf16[1,264,128]{2,1,0:T(8,128)(2,1)S(1)}, bf16[1,264,128]{2,1,0:T(8,128)(2,1)S(1)}, u32[]{:S(2)}, u32[]{:S(2)}) collective-permute-start(bf16[1,264,128]{2,1,0:T(8,128)(2,1)S(1)} %get-tuple-element.21), channel_id=1, source_target_pairs={{5,0},{4,1},{7,2},{6,3},{9,4},{8,5},{11,6},{10,7},{13,8},{12,9},{1... | collective-permute-start | bytes 202760 | tf_op jit(solution)/shard_map/ppermute | solution.py:29
  7.7 6.8 %collective-permute-start.3 = (bf16[1,264,128]{2,1,0:T(8,128)(2,1)S(1)}, bf16[1,264,128]{2,1,0:T(8,128)(2,1)S(1)}, u32[]{:S(2)}, u32[]{:S(2)}) collective-permute-start(bf16[1,264,128]{2,1,0:T(8,128)(2,1)S(1)} %get-tuple-element.21), channel_id=1, source_target_pairs={{4,0},{5,1},{6,2},{7,3},{8,4},{9,5},{10,6},{11,7},{12,8},{13,9},{1... | collective-permute-start | bytes 202760 | tf_op jit(solution)/shard_map/ppermute | solution.py:29
  8.8 5.7 %collective-permute-start = (bf16[1,264,128]{2,1,0:T(8,128)(2,1)S(1)}, bf16[1,264,128]{2,1,0:T(8,128)(2,1)S(1)}, u32[]{:S(2)}, u32[]{:S(2)}) collective-permute-start(bf16[1,264,128]{2,1,0:T(8,128)(2,1)S(1)} %get-tuple-element.21), channel_id=1, source_target_pairs={{1,0},{0,1},{3,2},{2,3},{5,4},{4,5},{7,6},{6,7},{9,8},{8,9},{11,10... | collective-permute-start | bytes 202760 | tf_op jit(solution)/shard_map/ppermute | solution.py:29
  9.3 5.3 %collective-permute-start.6 = (bf16[1,264,128]{2,1,0:T(8,128)(2,1)S(1)}, bf16[1,264,128]{2,1,0:T(8,128)(2,1)S(1)}, u32[]{:S(2)}, u32[]{:S(2)}) collective-permute-start(bf16[1,264,128]{2,1,0:T(8,128)(2,1)S(1)} %collective-permute-done.1.refs_1_), channel_id=1, source_target_pairs={{5,0},{4,1},{7,2},{6,3},{9,4},{8,5},{11,6},{10,7},{13,8},{12,9},{1... | collective-permute-start | bytes 202760 | tf_op jit(solution)/shard_map/ppermute | solution.py:29
  10.5 4.1 %collective-permute-start.5 = (bf16[1,264,128]{2,1,0:T(8,128)(2,1)S(1)}, bf16[1,264,128]{2,1,0:T(8,128)(2,1)S(1)}, u32[]{:S(2)}, u32[]{:S(2)}) collective-permute-start(bf16[1,264,128]{2,1,0:T(8,128)(2,1)S(1)} %collective-permute-done.1.refs_1_), channel_id=1, source_target_pairs={{4,0},{5,1},{6,2},{7,3},{8,4},{9,5},{10,6},{11,7},{12,8},{13,9},{1... | collective-permute-start | bytes 202760 | tf_op jit(solution)/shard_map/ppermute | solution.py:29
  12.2 4.3 %collective-permute-start.2 = (bf16[1,264,128]{2,1,0:T(8,128)(2,1)S(1)}, bf16[1,264,128]{2,1,0:T(8,128)(2,1)S(1)}, u32[]{:S(2)}, u32[]{:S(2)}) collective-permute-start(bf16[1,264,128]{2,1,0:T(8,128)(2,1)S(1)} %collective-permute-done.1.refs_1_), channel_id=1, source_target_pairs={{1,0},{0,1},{3,2},{2,3},{5,4},{4,5},{7,6},{6,7},{9,8},{8,9},{11,10... | collective-permute-start | bytes 202760 | tf_op jit(solution)/shard_map/ppermute | solution.py:29
  18.7 5.6 %collective-permute-start.10 = (bf16[1,264,128]{2,1,0:T(8,128)(2,1)S(1)}, bf16[1,264,128]{2,1,0:T(8,128)(2,1)S(1)}, u32[]{:S(2)}, u32[]{:S(2)}) collective-permute-start(bf16[1,264,128]{2,1,0:T(8,128)(2,1)S(1)} %get-tuple-element.29), channel_id=1, source_target_pairs={{0,5},{1,4},{2,7},{3,6},{4,9},{5,8},{6,11},{7,10},{8,13},{9,12},{1... | collective-permute-start | bytes 202760 | tf_op jit(solution)/shard_map/ppermute | solution.py:33
  18.7 6.2 %collective-permute-start.11 = (bf16[1,264,128]{2,1,0:T(8,128)(2,1)S(1)}, bf16[1,264,128]{2,1,0:T(8,128)(2,1)S(1)}, u32[]{:S(2)}, u32[]{:S(2)}) collective-permute-start(bf16[1,264,128]{2,1,0:T(8,128)(2,1)S(1)} %get-tuple-element.30), channel_id=1, source_target_pairs={{0,4},{1,5},{2,6},{3,7},{4,8},{5,9},{6,10},{7,11},{8,12},{9,13},{1... | collective-permute-start | bytes 202760 | tf_op jit(solution)/shard_map/ppermute | solution.py:33
  19.8 5.2 %collective-permute-start.12 = (bf16[1,264,128]{2,1,0:T(8,128)(2,1)S(1)}, bf16[1,264,128]{2,1,0:T(8,128)(2,1)S(1)}, u32[]{:S(2)}, u32[]{:S(2)}) collective-permute-start(bf16[1,264,128]{2,1,0:T(8,128)(2,1)S(1)} %get-tuple-element.31), channel_id=1, source_target_pairs={{0,1},{1,0},{2,3},{3,2},{4,5},{5,4},{6,7},{7,6},{8,9},{9,8},{10,11... | collective-permute-start | bytes 202760 | tf_op jit(solution)/shard_map/ppermute | solution.py:33
  20.8 7.8 %collective-permute-start.7 = (bf16[1,264,128]{2,1,0:T(8,128)(2,1)S(1)}, bf16[1,264,128]{2,1,0:T(8,128)(2,1)S(1)}, u32[]{:S(2)}, u32[]{:S(2)}) collective-permute-start(bf16[1,264,128]{2,1,0:T(8,128)(2,1)S(1)} %get-tuple-element.26), channel_id=1, source_target_pairs={{0,4},{1,5},{2,6},{3,7},{4,8},{5,9},{6,10},{7,11},{8,12},{9,13},{1... | collective-permute-start | bytes 202760 | tf_op jit(solution)/shard_map/ppermute | solution.py:33
  20.8 7.8 %collective-permute-start.8 = (bf16[1,264,128]{2,1,0:T(8,128)(2,1)S(1)}, bf16[1,264,128]{2,1,0:T(8,128)(2,1)S(1)}, u32[]{:S(2)}, u32[]{:S(2)}) collective-permute-start(bf16[1,264,128]{2,1,0:T(8,128)(2,1)S(1)} %get-tuple-element.27), channel_id=1, source_target_pairs={{0,5},{1,4},{2,7},{3,6},{4,9},{5,8},{6,11},{7,10},{8,13},{9,12},{1... | collective-permute-start | bytes 202760 | tf_op jit(solution)/shard_map/ppermute | solution.py:33
  24.2 4.7 %collective-permute-start.9 = (bf16[1,264,128]{2,1,0:T(8,128)(2,1)S(1)}, bf16[1,264,128]{2,1,0:T(8,128)(2,1)S(1)}, u32[]{:S(2)}, u32[]{:S(2)}) collective-permute-start(bf16[1,264,128]{2,1,0:T(8,128)(2,1)S(1)} %get-tuple-element.28), channel_id=1, source_target_pairs={{0,1},{1,0},{2,3},{3,2},{4,5},{5,4},{6,7},{7,6},{8,9},{9,8},{10,11... | collective-permute-start | bytes 202760 | tf_op jit(solution)/shard_map/ppermute | solution.py:33
  25.0 5.6 %collective-permute-start.13 = (bf16[1,264,128]{2,1,0:T(8,128)(2,1)S(1)}, bf16[1,264,128]{2,1,0:T(8,128)(2,1)S(1)}, u32[]{:S(2)}, u32[]{:S(2)}) collective-permute-start(bf16[1,264,128]{2,1,0:T(8,128)(2,1)S(1)} %shard_map.40), channel_id=1, source_target_pairs={{0,2},{1,3},{2,0},{3,1},{4,6},{5,7},{6,4},{7,5},{8,10},{9,11},{10,... | collective-permute-start | bytes 202760 | tf_op jit(solution)/shard_map/ppermute | solution.py:33
